TPU v7x, 128 devices: a whole 4x4x4 slice. The times are simulated.
128 devices in a mesh: pod: 1, dp: 2 (over core), ep: 64 (over z, y, x).
Axes of the slice: x: 4, y: 4, z: 4, core: 2. Of those that a mesh axis runs over, the one named last changes fastest.
Arguments:
- x_start: bfloat16 [32768, 512], P(('pod', 'dp', 'ep'))
- route_a: int32 [32768, 6], P(('pod', 'dp', 'ep'))
- route_b: int32 [32768, 6], P(('pod', 'dp', 'ep'))
- gate_a: float32 [32768, 6], P(('pod', 'dp', 'ep'))
- gate_b: float32 [32768, 6], P(('pod', 'dp', 'ep'))
- grad_out: bfloat16 [32768, 512], P(('pod', 'dp', 'ep'))
- w1_a: bfloat16 [64, 512, 384], P('ep')
- w3_a: bfloat16 [64, 512, 384], P('ep')
- w2_a: bfloat16 [64, 384, 512], P('ep')
- w1_b: bfloat16 [64, 512, 384], P('ep')
- w3_b: bfloat16 [64, 512, 384], P('ep')
- w2_b: bfloat16 [64, 384, 512], P('ep')
Outputs:
- output 1: bfloat16 [32768, 512], P(('pod', 'dp', 'ep'))
- output 2: bfloat16 [32768, 512], P(('pod', 'dp', 'ep'))
- output 3: float32 [64, 512, 384], P(('pod', 'ep'), 'dp')
- output 4: float32 [64, 512, 384], P(('pod', 'ep'), 'dp')
- output 5: float32 [64, 384, 512], P(('pod', 'ep'), 'dp')
- output 6: float32 [64, 512, 384], P(('pod', 'ep'), 'dp')
- output 7: float32 [64, 512, 384], P(('pod', 'ep'), 'dp')
- output 8: float32 [64, 384, 512], P(('pod', 'ep'), 'dp')
- output 9: float32 [32768, 6], P(('pod', 'dp', 'ep'))
- output 10: float32 [32768, 6], P(('pod', 'dp', 'ep'))
All inputs are finite; a program needn't handle non-finite values.
Results may differ from a plain program's by a relative error of at most 0.00763038.
Values are sent between devices in bfloat16 or wider.
A program may use at most 1 GiB of HBM per device.

v0:
```python
import jax
import jax.numpy as jnp
from jax import lax
from jax.sharding import PartitionSpec as P


def route_rows(expert_ids, n_experts, capacity):
    n_tokens, top_k = expert_ids.shape
    flat_ids = expert_ids.reshape(-1)
    onehot = (flat_ids[:, None] == jnp.arange(n_experts, dtype=jnp.int32)[None, :]).astype(jnp.int32)
    earlier = jnp.cumsum(onehot, axis=0) - onehot
    slot_idx = jnp.sum(earlier * onehot, axis=1)
    pair_row = flat_ids * capacity + slot_idx
    pair_tok = jnp.arange(n_tokens * top_k, dtype=jnp.int32) // top_k
    row_tok = jnp.zeros((n_experts * capacity,), jnp.int32).at[pair_row].set(pair_tok)
    row_used = jnp.zeros((n_experts * capacity,), jnp.bfloat16).at[pair_row].set(1.0)
    return pair_row, row_tok, row_used


def take_rows(values, row_tok, row_used):
    return jnp.take(values, row_tok, axis=0) * row_used[:, None]


def place_gates(gate_vals, pair_row, n_rows):
    return jnp.zeros((n_rows,), jnp.float32).at[pair_row].set(gate_vals.reshape(-1))


def mix_back(x_in, out_rows, pair_row, gate_vals):
    n_tokens, top_k = gate_vals.shape
    pair_out = jnp.take(out_rows, pair_row, axis=0).reshape(n_tokens, top_k, -1)
    mixed_sum = jnp.sum(gate_vals[:, :, None] * pair_out, axis=1)
    return (x_in.astype(jnp.float32) + mixed_sum).astype(jnp.bfloat16)


def add_back(grad_in, du_rows, pair_row, gate_grad_rows, top_k):
    n_tokens = grad_in.shape[0]
    pair_grad = jnp.take(du_rows, pair_row, axis=0).reshape(n_tokens, top_k, -1)
    grad_x = (grad_in.astype(jnp.float32) + jnp.sum(pair_grad, axis=1, dtype=jnp.float32)).astype(jnp.bfloat16)
    return grad_x, jnp.take(gate_grad_rows, pair_row, axis=0).reshape(n_tokens, top_k)


def expert_forward(recv_rows, w_up1, w_up3, w_down):
    pre_one = jnp.einsum('secd,edf->escf', recv_rows, w_up1, preferred_element_type=jnp.float32)
    pre_three = jnp.einsum('secd,edf->escf', recv_rows, w_up3, preferred_element_type=jnp.float32)
    hidden = (jax.nn.silu(pre_one) * pre_three).astype(jnp.bfloat16)
    return jnp.einsum('escf,efd->secd', hidden, w_down, preferred_element_type=jnp.float32).astype(jnp.bfloat16)


def expert_backward(recv_rows, recv_dy, recv_gate, w_up1, w_up3, w_down):
    pre_one = jnp.einsum('secd,edf->escf', recv_rows, w_up1, preferred_element_type=jnp.float32)
    pre_three = jnp.einsum('secd,edf->escf', recv_rows, w_up3, preferred_element_type=jnp.float32)
    sig_one = jax.nn.sigmoid(pre_one)
    act_one = pre_one * sig_one
    hidden = (act_one * pre_three).astype(jnp.bfloat16)
    back_proj = jnp.einsum('secd,efd->escf', recv_dy, w_down, preferred_element_type=jnp.float32)
    gate_grad = jnp.sum(back_proj * hidden, axis=-1)
    gate_esc = jnp.transpose(recv_gate, (1, 0, 2))
    scaled_dy = (recv_gate[..., None] * recv_dy).astype(jnp.bfloat16)
    dw_down = jnp.einsum('escf,secd->efd', hidden, scaled_dy, preferred_element_type=jnp.float32)
    d_hidden = gate_esc[..., None] * back_proj
    d_pre_one = (d_hidden * pre_three * sig_one * (1.0 + pre_one * (1.0 - sig_one))).astype(jnp.bfloat16)
    d_pre_three = (d_hidden * act_one).astype(jnp.bfloat16)
    dw_up1 = jnp.einsum('secd,escf->edf', recv_rows, d_pre_one, preferred_element_type=jnp.float32)
    dw_up3 = jnp.einsum('secd,escf->edf', recv_rows, d_pre_three, preferred_element_type=jnp.float32)
    grad_rows = (jnp.einsum('escf,edf->secd', d_pre_one, w_up1, preferred_element_type=jnp.float32)
                 + jnp.einsum('escf,edf->secd', d_pre_three, w_up3, preferred_element_type=jnp.float32)).astype(jnp.bfloat16)
    return grad_rows, jnp.transpose(gate_grad, (1, 0, 2)), dw_up1, dw_up3, dw_down


def solution(mesh):
    n_ep = mesh.shape['ep']
    tok_spec = P(('pod', 'dp', 'ep'), None)
    weight_spec = P('ep', None, None)
    grad_spec = P(('pod', 'ep'), 'dp', None)

    def local_step(x_start, route_a, route_b, gate_a, gate_b, grad_out, w1_a, w3_a, w2_a, w1_b, w3_b, w2_b):
        n_tokens = x_start.shape[0]
        top_k = route_a.shape[1]
        n_local = w1_a.shape[0]
        n_experts = n_local * n_ep
        capacity = 3 * n_tokens * top_k // (2 * n_experts)
        n_rows = n_experts * capacity

        def exchange(send_rows):
            shaped = send_rows.reshape((n_ep, n_local, capacity) + send_rows.shape[1:])
            return lax.all_to_all(shaped, 'ep', 0, 0)

        def give_back(expert_rows):
            returned = lax.all_to_all(expert_rows, 'ep', 0, 0)
            return returned.reshape((n_rows,) + expert_rows.shape[3:])

        def layer_backward(recv_rows, grad_in, route_plan, gate_vals, w_up1, w_up3, w_down):
            pair_row, row_tok, row_used = route_plan
            recv_dy = exchange(take_rows(grad_in, row_tok, row_used))
            recv_gate = exchange(place_gates(gate_vals, pair_row, n_rows))
            grad_rows, gate_grad, dw_up1, dw_up3, dw_down = expert_backward(recv_rows, recv_dy, recv_gate, w_up1, w_up3, w_down)
            grad_x, gate_out = add_back(grad_in, give_back(grad_rows), pair_row, give_back(gate_grad), top_k)
            dw_parts = [lax.psum_scatter(grad_part, 'dp', scatter_dimension=1, tiled=True) for grad_part in (dw_up1, dw_up3, dw_down)]
            return grad_x, gate_out, dw_parts[0], dw_parts[1], dw_parts[2]

        plan_a = route_rows(route_a, n_experts, capacity)
        plan_b = route_rows(route_b, n_experts, capacity)
        recv_a = exchange(take_rows(x_start, plan_a[1], plan_a[2]))
        x_mid = mix_back(x_start, give_back(expert_forward(recv_a, w1_a, w3_a, w2_a)), plan_a[0], gate_a)
        recv_b = exchange(take_rows(x_mid, plan_b[1], plan_b[2]))
        x_final = mix_back(x_mid, give_back(expert_forward(recv_b, w1_b, w3_b, w2_b)), plan_b[0], gate_b)
        x_kept, recv_b_kept, grad_kept = lax.optimization_barrier((x_start, recv_b, grad_out))
        grad_mid, dgate_b, dw1_b, dw3_b, dw2_b = layer_backward(recv_b_kept, grad_kept, plan_b, gate_b, w1_b, w3_b, w2_b)
        recv_a_again = exchange(take_rows(x_kept, plan_a[1], plan_a[2]))
        grad_x, dgate_a, dw1_a, dw3_a, dw2_a = layer_backward(recv_a_again, grad_mid, plan_a, gate_a, w1_a, w3_a, w2_a)
        return (x_final, grad_x, dw1_a, dw3_a, dw2_a, dw1_b, dw3_b, dw2_b, dgate_a, dgate_b)

    return jax.shard_map(local_step, mesh=mesh,
                         in_specs=(tok_spec,) * 6 + (weight_spec,) * 6,
                         out_specs=(tok_spec, tok_spec) + (grad_spec,) * 6 + (tok_spec, tok_spec),
                         check_vma=False)
```

profile of v0, /device:TPU:2, one launch (start us, length us, event | category | flops | bytes accessed | tf_op | source)
XLA Modules:
  0.0 706.1 jit_solution(13442839591808321980)
XLA Ops:
  9.4 18.1 %reduce-window.14 = s32[64,12,128]{2,1,0:T(8,128)S(1)} reduce-window(s32[64,12,128]{2,1,0:T(8,128)S(1)} %fusion.74, s32[]{:T(128)} %constant.35.clone.1), window={size=1x1x128 pad=0_0x0_0x127_0}, to_apply=%region_0.0 | reduce-window | flops 12484608 | bytes 786436 | tf_op jit(solution)/shard_map/reduce-window
  34.9 11.1 %scatter_custom_fusion.1 = bf16[2304]{0:T(1024)(128)(2,1)S(1)} fusion(s32[1536]{0:T(1024)S(1)} %fusion.105, bf16[1536]{0:T(1024)(128)(2,1)S(1)} %broadcast.143, bf16[]{:T(256)} %constant.47.clone.1), kind=kCustom, calls=%fused_computation.175 | custom fusion | bytes 4610 | tf_op jit(solution)/shard_map/scatter | solution.py:16
  59.1 49.7 %all_to_all.65 = bf16[64,1,36,512]{3,2,1,0:T(8,128)(2,1)S(1)} all-to-all(bf16[64,1,36,512]{3,2,1,0:T(8,128)(2,1)S(1)} %bitcast.209), channel_id=1, replica_groups=mesh['pod'=1,'dp'=2,'ep'=64] {'ep'}, dimensions={0} | all-to-all | bytes 4718592 | tf_op jit(solution)/shard_map/all_to_all | solution.py:86
  122.2 9.1 %all-to-all-start.1 = ((bf16[64,1,36,512]{3,2,1,0:T(8,128)(2,1)}), bf16[64,1,36,512]{3,2,1,0:T(8,128)(2,1)}, u32[]{:S(2)}, u32[]{:S(2)}) async-start(bf16[64,1,36,512]{3,2,1,0:T(8,128)(2,1)} %copy.61), calls=%async_computation.1 | async-start | bytes 5242880 | tf_op jit(solution)/shard_map/all_to_all | solution.py:89
  132.1 18.1 %reduce-window.16 = s32[64,12,128]{2,1,0:T(8,128)S(1)} reduce-window(s32[64,12,128]{2,1,0:T(8,128)S(1)} %fusion.75, s32[]{:T(128)} %constant.35.clone.1), window={size=1x1x128 pad=0_0x0_0x127_0}, to_apply=%region_6.9 | reduce-window | flops 12484608 | bytes 786436 | tf_op jit(solution)/shard_map/reduce-window.2
  151.9 23.9 %scatter_custom_fusion.3 = bf16[2304]{0:T(1024)(128)(2,1)S(1)} fusion(s32[1536]{0:T(1024)S(1)} %fusion.106, bf16[1536]{0:T(1024)(128)(2,1)S(1)} %broadcast.143, bf16[]{:T(256)} %constant.47.clone.1), kind=kCustom, calls=%fused_computation.173 | custom fusion | bytes 4610 | tf_op jit(solution)/shard_map/scatter | solution.py:16
  202.6 7.5 %gather_fusion.2 = bf16[2304,512]{1,0:T(8,128)(2,1)} fusion(bf16[256,512]{1,0:T(8,128)(2,1)S(1)} %add_convert_fusion.5, s32[3072]{0:T(1024)S(1)} %pad_clamp_fusion), kind=kCustom, calls=%fused_computation.3.clone | custom fusion | bytes 4727808 | tf_op jit(solution)/shard_map/jit(_take)/gather | solution.py:21
  215.3 10.6 %all-to-all-start.2 = ((bf16[64,1,36,512]{3,2,1,0:T(8,128)(2,1)}), bf16[64,1,36,512]{3,2,1,0:T(8,128)(2,1)}, u32[]{:S(2)}, u32[]{:S(2)}) async-start(bf16[64,1,36,512]{3,2,1,0:T(8,128)(2,1)} %bitcast.208), calls=%async_computation.2 | async-start | bytes 5242880 | tf_op jit(solution)/shard_map/all_to_all | solution.py:86
  233.1 29.2 %all-to-all-done.2 = bf16[64,1,36,512]{3,2,1,0:T(8,128)(2,1)} async-done(((bf16[64,1,36,512]{3,2,1,0:T(8,128)(2,1)}), bf16[64,1,36,512]{3,2,1,0:T(8,128)(2,1)}, u32[]{:S(2)}, u32[]{:S(2)}) %all-to-all-start.2) | async-done | bytes 2359328 | tf_op jit(solution)/shard_map/all_to_all | solution.py:86
  262.4 9.8 %all-to-all-start.4 = ((f32[64,1,36]{2,1,0:T(1,128)}), f32[64,1,36]{2,1,0:T(1,128)}, u32[]{:S(2)}, u32[]{:S(2)}) async-start(f32[64,1,36]{2,1,0:T(1,128)} %bitcast.26), calls=%async_computation.4 | async-start | bytes 65536 | tf_op jit(solution)/shard_map/all_to_all | solution.py:86
  272.2 7.5 %gather_fusion.4 = bf16[2304,512]{1,0:T(8,128)(2,1)} fusion(bf16[256,512]{1,0:T(8,128)(2,1)S(1)} %copy-done.3, s32[3072]{0:T(1024)S(1)} %pad_clamp_fusion), kind=kCustom, calls=%fused_computation.4.clone | custom fusion | bytes 4727808 | tf_op jit(solution)/shard_map/jit(_take)/gather | solution.py:21
  284.7 10.6 %all-to-all-start.5 = ((bf16[64,1,36,512]{3,2,1,0:T(8,128)(2,1)}), bf16[64,1,36,512]{3,2,1,0:T(8,128)(2,1)}, u32[]{:S(2)}, u32[]{:S(2)}) async-start(bf16[64,1,36,512]{3,2,1,0:T(8,128)(2,1)} %bitcast.207), calls=%async_computation.5 | async-start | bytes 5242880 | tf_op jit(solution)/shard_map/all_to_all | solution.py:86
  300.3 7.2 %convert_bitcast_fusion = bf16[64,1,36,512]{3,0,2,1:T(8,128)(2,1)} fusion(f32[64,36,384]{2,0,1:T(8,128)} %fusion.18, bf16[64,1,36,512]{3,2,1,0:T(8,128)(2,1)} %all-to-all-done.2, bf16[1,384,512]{2,1,0:T(8,128)(2,1)S(1)} %copy-done, bf16[1,512,384]{2,1,0:T(8,128)(2,1)S(1)} %copy-done.11), kind=kOutput, calls=%fused_computation.72 | convolution fusion | flops 1818427392 | bytes 9043968 | tf_op jit(solution)/shard_map/escf,efd->secd/dot_general | solution.py:46
  312.1 21.1 %all-to-all-done.5 = bf16[64,1,36,512]{3,2,1,0:T(8,128)(2,1)} async-done(((bf16[64,1,36,512]{3,2,1,0:T(8,128)(2,1)}), bf16[64,1,36,512]{3,2,1,0:T(8,128)(2,1)}, u32[]{:S(2)}, u32[]{:S(2)}) %all-to-all-start.5) | async-done | bytes 2359328 | tf_op jit(solution)/shard_map/all_to_all | solution.py:86
  333.2 10.2 %all-to-all-start.3 = ((bf16[64,1,36,512]{3,2,1,0:T(8,128)(2,1)}), bf16[64,1,36,512]{3,2,1,0:T(8,128)(2,1)}, u32[]{:S(2)}, u32[]{:S(2)}) async-start(bf16[64,1,36,512]{3,2,1,0:T(8,128)(2,1)} %copy.70), calls=%async_computation.3 | async-start | bytes 5242880 | tf_op jit(solution)/shard_map/all_to_all | solution.py:89
  350.5 7.2 %multiply_reduce_fusion.2 = (f32[64,36]{0,1:T(8,128)S(1)}, bf16[64,36,384]{2,0,1:T(8,128)(2,1)}, bf16[64,36,384]{2,0,1:T(8,128)(2,1)S(1)}, bf16[64,36,384]{2,0,1:T(8,128)(2,1)}) fusion(f32[64,36,384]{2,0,1:T(8,128)S(1)} %fusion.38, f32[64,36,384]{2,0,1:T(8,128)S(1)} %fusion.36, f32[64,36]{0,1:T(8,128)S(1)} %copy.73, bf16[1,384,512]{2,1,0:T(8,128)(2,1)S(1)} %copy-done, ...), kind=kOutput, calls=%fused_computation.23 | convolution fusion | flops 922777344 | bytes 15157248 | tf_op jit(solution)/shard_map/secd,efd->escf/dot_general | solution.py:55
  363.1 18.1 %all-to-all-done.3 = bf16[64,1,36,512]{3,2,1,0:T(8,128)(2,1)} async-done(((bf16[64,1,36,512]{3,2,1,0:T(8,128)(2,1)}), bf16[64,1,36,512]{3,2,1,0:T(8,128)(2,1)}, u32[]{:S(2)}, u32[]{:S(2)}) %all-to-all-start.3) | async-done | bytes 2359328 | tf_op jit(solution)/shard_map/all_to_all | solution.py:89
  381.2 8.7 %all-to-all-start.12 = ((f32[64,1,36]{2,1,0:T(1,128)}), f32[64,1,36]{2,1,0:T(1,128)S(1)}, u32[]{:S(2)}, u32[]{:S(2)}) async-start(f32[64,1,36]{2,1,0:T(1,128)} %copy.92), calls=%async_computation.18 | async-start | bytes 65536 | tf_op jit(solution)/shard_map/all_to_all | solution.py:89
  398.4 9.7 %all-to-all-start.6 = ((bf16[64,1,36,512]{3,2,1,0:T(8,128)(2,1)}), bf16[64,1,36,512]{3,2,1,0:T(8,128)(2,1)}, u32[]{:S(2)}, u32[]{:S(2)}) async-start(bf16[64,1,36,512]{3,2,1,0:T(8,128)(2,1)} %copy.78), calls=%async_computation.6 | async-start | bytes 5242880 | tf_op jit(solution)/shard_map/all_to_all | solution.py:89
  415.4 7.5 %gather_fusion.7 = bf16[2304,512]{1,0:T(8,128)(2,1)} fusion(bf16[256,512]{1,0:T(8,128)(2,1)S(1)} %copy-done.2, s32[3072]{0:T(1024)S(1)} %pad_clamp_fusion.1), kind=kCustom, calls=%fused_computation.6.clone | custom fusion | bytes 4727808 | tf_op jit(solution)/shard_map/jit(_take)/gather | solution.py:21
  433.0 8.4 %gather_fusion.10 = f32[1536]{0:T(1024)S(1)} fusion(f32[2304]{0:T(1024)S(1)} %reshape.405, s32[2048]{0:T(1024)S(1)} %pad_clamp_fusion.2), kind=kCustom, calls=%fused_computation.10.clone | custom fusion | bytes 18432 | tf_op jit(solution)/shard_map/jit(_take)/gather | solution.py:39
  446.7 8.9 %all-to-all-start.7 = ((f32[64,1,36]{2,1,0:T(1,128)}), f32[64,1,36]{2,1,0:T(1,128)S(1)}, u32[]{:S(2)}, u32[]{:S(2)}) async-start(f32[64,1,36]{2,1,0:T(1,128)} %bitcast.34), calls=%async_computation.7 | async-start | bytes 65536 | tf_op jit(solution)/shard_map/all_to_all | solution.py:86
  477.7 7.5 %gather_fusion.6 = bf16[2304,512]{1,0:T(8,128)(2,1)} fusion(bf16[256,512]{1,0:T(8,128)(2,1)S(1)} %add_convert_fusion.3, s32[3072]{0:T(1024)S(1)} %pad_clamp_fusion.1), kind=kCustom, calls=%fused_computation.5.clone | custom fusion | bytes 4727808 | tf_op jit(solution)/shard_map/jit(_take)/gather | solution.py:21
  491.7 10.3 %all-to-all-start.9 = ((bf16[64,1,36,512]{3,2,1,0:T(8,128)(2,1)}), bf16[64,1,36,512]{3,2,1,0:T(8,128)(2,1)S(1)}, u32[]{:S(2)}, u32[]{:S(2)}) async-start(bf16[64,1,36,512]{3,2,1,0:T(8,128)(2,1)} %bitcast.205), calls=%async_computation.9 | async-start | bytes 5242880 | tf_op jit(solution)/shard_map/all_to_all | solution.py:86
  516.3 24.2 %all-to-all-done.9 = bf16[64,1,36,512]{3,2,1,0:T(8,128)(2,1)S(1)} async-done(((bf16[64,1,36,512]{3,2,1,0:T(8,128)(2,1)}), bf16[64,1,36,512]{3,2,1,0:T(8,128)(2,1)S(1)}, u32[]{:S(2)}, u32[]{:S(2)}) %all-to-all-start.9) | async-done | bytes 2359328 | tf_op jit(solution)/shard_map/all_to_all | solution.py:86
  540.5 7.9 %all-to-all-start.8 = ((bf16[64,1,36,512]{3,2,1,0:T(8,128)(2,1)}), bf16[64,1,36,512]{3,2,1,0:T(8,128)(2,1)}, u32[]{:S(2)}, u32[]{:S(2)}) async-start(bf16[64,1,36,512]{3,2,1,0:T(8,128)(2,1)} %bitcast.206), calls=%async_computation.8 | async-start | bytes 5242880 | tf_op jit(solution)/shard_map/all_to_all | solution.py:86
  561.4 23.8 %all-to-all-done.8 = bf16[64,1,36,512]{3,2,1,0:T(8,128)(2,1)} async-done(((bf16[64,1,36,512]{3,2,1,0:T(8,128)(2,1)}), bf16[64,1,36,512]{3,2,1,0:T(8,128)(2,1)}, u32[]{:S(2)}, u32[]{:S(2)}) %all-to-all-start.8) | async-done | bytes 2359328 | tf_op jit(solution)/shard_map/all_to_all | solution.py:86
  588.0 8.7 %multiply_reduce_fusion.3 = (f32[64,36]{0,1:T(8,128)}, bf16[64,36,384]{2,0,1:T(8,128)(2,1)S(1)}, bf16[64,36,384]{2,0,1:T(8,128)(2,1)}, bf16[64,36,384]{2,0,1:T(8,128)(2,1)}) fusion(f32[64,36,384]{2,0,1:T(8,128)} %fusion.12, f32[64,36,384]{2,0,1:T(8,128)S(1)} %copy-done.8, f32[64,36]{0,1:T(8,128)S(1)} %copy-done.31, bf16[1,384,512]{2,1,0:T(8,128)(2,1)S(1)} %copy-done.35, ...), kind=kOutput, calls=%fused_computation.24 | convolution fusion | flops 922777344 | bytes 15157248 | tf_op jit(solution)/shard_map/secd,efd->escf/dot_general | solution.py:55
  600.3 10.5 %all-to-all-start.11 = ((f32[64,1,36]{2,1,0:T(1,128)}), f32[64,1,36]{2,1,0:T(1,128)}, u32[]{:S(2)}, u32[]{:S(2)}) async-start(f32[64,1,36]{2,1,0:T(1,128)} %copy.91), calls=%async_computation.17 | async-start | bytes 65536 | tf_op jit(solution)/shard_map/all_to_all | solution.py:89
  626.0 10.6 %all-to-all-start.10 = ((bf16[64,1,36,512]{3,2,1,0:T(8,128)(2,1)}), bf16[64,1,36,512]{3,2,1,0:T(8,128)(2,1)}, u32[]{:S(2)}, u32[]{:S(2)}) async-start(bf16[64,1,36,512]{3,2,1,0:T(8,128)(2,1)} %copy.86), calls=%async_computation.10 | async-start | bytes 5242880 | tf_op jit(solution)/shard_map/all_to_all | solution.py:89
  652.1 8.4 %gather_fusion.9 = f32[1536]{0:T(1024)S(1)} fusion(f32[2304]{0:T(1024)S(1)} %reshape.403, s32[2048]{0:T(1024)S(1)} %copy-done.18), kind=kCustom, calls=%fused_computation.2.clone | custom fusion | bytes 18432 | tf_op jit(solution)/shard_map/jit(_take)/gather | solution.py:39
  661.3 16.6 %all-to-all-done.10 = bf16[64,1,36,512]{3,2,1,0:T(8,128)(2,1)} async-done(((bf16[64,1,36,512]{3,2,1,0:T(8,128)(2,1)}), bf16[64,1,36,512]{3,2,1,0:T(8,128)(2,1)}, u32[]{:S(2)}, u32[]{:S(2)}) %all-to-all-start.10) | async-done | bytes 2359328 | tf_op jit(solution)/shard_map/all_to_all | solution.py:89
  (219 shorter events, 250.1 us)
Async XLA Ops:
  7.2 293.1 %copy-start = (bf16[1,384,512]{2,1,0:T(8,128)(2,1)S(1)}, bf16[1,384,512]{2,1,0:T(8,128)(2,1)}, u32[]{:S(2)}) copy-start(bf16[1,384,512]{2,1,0:T(8,128)(2,1)} %param.29) | copy-start | bytes 1179652
  9.4 36.6 %copy-start.2 = (bf16[256,512]{1,0:T(8,128)(2,1)S(1)}, bf16[256,512]{1,0:T(8,128)(2,1)}, u32[]{:S(2)}) copy-start(bf16[256,512]{1,0:T(8,128)(2,1)} %param.18) | copy-start | bytes 786436
  28.6 24.4 %copy-start.34 = (s32[1536]{0:T(1024)}, s32[1536]{0:T(1024)S(1)}, u32[]{:S(2)}) copy-start(s32[1536]{0:T(1024)S(1)} %fusion.105) | copy-start | bytes 18436
  34.8 18.1 %copy-start.28 = (pred[2304]{0:T(1024)(128)(4,1)}, pred[2304]{0:T(1024)(128)(4,1)S(1)}, u32[]{:S(2)}) copy-start(pred[2304]{0:T(1024)(128)(4,1)S(1)} %compare_and_fusion.1) | copy-start | bytes 6916
  59.1 51.2 %copy-start.6 = (bf16[1,512,384]{2,1,0:T(8,128)(2,1)S(1)}, bf16[1,512,384]{2,1,0:T(8,128)(2,1)}, u32[]{:S(2)}) copy-start(bf16[1,512,384]{2,1,0:T(8,128)(2,1)} %param.25) | copy-start | bytes 1179652
  122.2 60.0 %all-to-all-start.1 = ((bf16[64,1,36,512]{3,2,1,0:T(8,128)(2,1)}), bf16[64,1,36,512]{3,2,1,0:T(8,128)(2,1)}, u32[]{:S(2)}, u32[]{:S(2)}) async-start(bf16[64,1,36,512]{3,2,1,0:T(8,128)(2,1)} %copy.61), calls=%async_computation.1 | async-start | bytes 5242880 | tf_op jit(solution)/shard_map/all_to_all | solution.py:89
  131.6 19.5 %copy-start.19 = (s32[1536]{0:T(1024)}, s32[1536]{0:T(1024)S(1)}, u32[]{:S(2)}) copy-start(s32[1536]{0:T(1024)S(1)} %eq.58) | copy-start | bytes 18436
  132.1 49.9 %copy-start.32 = (f32[256,6]{0,1:T(8,128)S(1)}, f32[256,6]{0,1:T(8,128)}, u32[]{:S(2)}) copy-start(f32[256,6]{0,1:T(8,128)} %param.21) | copy-start | bytes 18436
  175.7 34.4 %copy-start.25 = (bf16[2304]{0:T(1024)(128)(2,1)}, bf16[2304]{0:T(1024)(128)(2,1)S(1)}, u32[]{:S(2)}) copy-start(bf16[2304]{0:T(1024)(128)(2,1)S(1)} %scatter_custom_fusion.3) | copy-start | bytes 13828
  182.2 27.9 %copy-start.30 = (pred[2304]{0:T(1024)(128)(4,1)}, pred[2304]{0:T(1024)(128)(4,1)S(1)}, u32[]{:S(2)}) copy-start(pred[2304]{0:T(1024)(128)(4,1)S(1)} %compare_and_fusion) | copy-start | bytes 6916
  215.3 56.9 %copy-start.3 = (bf16[256,512]{1,0:T(8,128)(2,1)S(1)}, bf16[256,512]{1,0:T(8,128)(2,1)}, u32[]{:S(2)}) copy-start(bf16[256,512]{1,0:T(8,128)(2,1)} %param.23) | copy-start | bytes 786436
  215.3 47.1 %all-to-all-start.2 = ((bf16[64,1,36,512]{3,2,1,0:T(8,128)(2,1)}), bf16[64,1,36,512]{3,2,1,0:T(8,128)(2,1)}, u32[]{:S(2)}, u32[]{:S(2)}) async-start(bf16[64,1,36,512]{3,2,1,0:T(8,128)(2,1)} %bitcast.208), calls=%async_computation.2 | async-start | bytes 5242880 | tf_op jit(solution)/shard_map/all_to_all | solution.py:86
  226.1 46.1 %copy-start.12 = (f32[256,6]{1,0:T(8,128)}, f32[256,6]{1,0:T(8,128)S(1)}, u32[]{:S(2)}) copy-start(f32[256,6]{1,0:T(8,128)S(1)} %copy.62) | copy-start | bytes 18436
  262.4 22.3 %all-to-all-start.4 = ((f32[64,1,36]{2,1,0:T(1,128)}), f32[64,1,36]{2,1,0:T(1,128)}, u32[]{:S(2)}, u32[]{:S(2)}) async-start(f32[64,1,36]{2,1,0:T(1,128)} %bitcast.26), calls=%async_computation.4 | async-start | bytes 65536 | tf_op jit(solution)/shard_map/all_to_all | solution.py:86
  284.7 48.5 %all-to-all-start.5 = ((bf16[64,1,36,512]{3,2,1,0:T(8,128)(2,1)}), bf16[64,1,36,512]{3,2,1,0:T(8,128)(2,1)}, u32[]{:S(2)}, u32[]{:S(2)}) async-start(bf16[64,1,36,512]{3,2,1,0:T(8,128)(2,1)} %bitcast.207), calls=%async_computation.5 | async-start | bytes 5242880 | tf_op jit(solution)/shard_map/all_to_all | solution.py:86
  333.2 48.1 %all-to-all-start.3 = ((bf16[64,1,36,512]{3,2,1,0:T(8,128)(2,1)}), bf16[64,1,36,512]{3,2,1,0:T(8,128)(2,1)}, u32[]{:S(2)}, u32[]{:S(2)}) async-start(bf16[64,1,36,512]{3,2,1,0:T(8,128)(2,1)} %copy.70), calls=%async_computation.3 | async-start | bytes 5242880 | tf_op jit(solution)/shard_map/all_to_all | solution.py:89
  381.2 17.2 %all-to-all-start.12 = ((f32[64,1,36]{2,1,0:T(1,128)}), f32[64,1,36]{2,1,0:T(1,128)S(1)}, u32[]{:S(2)}, u32[]{:S(2)}) async-start(f32[64,1,36]{2,1,0:T(1,128)} %copy.92), calls=%async_computation.18 | async-start | bytes 65536 | tf_op jit(solution)/shard_map/all_to_all | solution.py:89
  397.1 18.2 %copy-start.20 = (s32[1536]{0:T(1024)S(1)}, s32[1536]{0:T(1024)}, u32[]{:S(2)}) copy-start(s32[1536]{0:T(1024)} %copy-done.19) | copy-start | bytes 18436
  397.1 18.2 %copy-start.22 = (s32[1536]{0:T(1024)S(1)}, s32[1536]{0:T(1024)}, u32[]{:S(2)}) copy-start(s32[1536]{0:T(1024)} %copy-done.21) | copy-start | bytes 18436
  398.4 48.3 %all-to-all-start.6 = ((bf16[64,1,36,512]{3,2,1,0:T(8,128)(2,1)}), bf16[64,1,36,512]{3,2,1,0:T(8,128)(2,1)}, u32[]{:S(2)}, u32[]{:S(2)}) async-start(bf16[64,1,36,512]{3,2,1,0:T(8,128)(2,1)} %copy.78), calls=%async_computation.6 | async-start | bytes 5242880 | tf_op jit(solution)/shard_map/all_to_all | solution.py:89
  446.7 45.0 %all-to-all-start.7 = ((f32[64,1,36]{2,1,0:T(1,128)}), f32[64,1,36]{2,1,0:T(1,128)S(1)}, u32[]{:S(2)}, u32[]{:S(2)}) async-start(f32[64,1,36]{2,1,0:T(1,128)} %bitcast.34), calls=%async_computation.7 | async-start | bytes 65536 | tf_op jit(solution)/shard_map/all_to_all | solution.py:86
  491.7 56.7 %copy-start.16 = (f32[64,1,36]{2,1,0:T(1,128)}, f32[64,1,36]{2,1,0:T(1,128)S(1)}, u32[]{:S(2)}) copy-start(f32[64,1,36]{2,1,0:T(1,128)S(1)} %all-to-all-done.7) | copy-start | bytes 27652
  491.7 48.8 %all-to-all-start.9 = ((bf16[64,1,36,512]{3,2,1,0:T(8,128)(2,1)}), bf16[64,1,36,512]{3,2,1,0:T(8,128)(2,1)S(1)}, u32[]{:S(2)}, u32[]{:S(2)}) async-start(bf16[64,1,36,512]{3,2,1,0:T(8,128)(2,1)} %bitcast.205), calls=%async_computation.9 | async-start | bytes 5242880 | tf_op jit(solution)/shard_map/all_to_all | solution.py:86
  502.0 197.0 %reduce-scatter.17.cloned.1.call-start = ((), (), s32[]{:S(2)}) async-start(), calls=%async_computation.24 | async-start | bytes 1179648 | tf_op jit(solution)/shard_map/reduce_scatter | solution.py:98
  506.6 192.4 %reduce-scatter.13.cloned.1.call-start = ((), (), s32[]{:S(2)}) async-start(), calls=%async_computation.22 | async-start | bytes 1179648 | tf_op jit(solution)/shard_map/reduce_scatter | solution.py:98
  540.5 44.6 %all-to-all-start.8 = ((bf16[64,1,36,512]{3,2,1,0:T(8,128)(2,1)}), bf16[64,1,36,512]{3,2,1,0:T(8,128)(2,1)}, u32[]{:S(2)}, u32[]{:S(2)}) async-start(bf16[64,1,36,512]{3,2,1,0:T(8,128)(2,1)} %bitcast.206), calls=%async_computation.8 | async-start | bytes 5242880 | tf_op jit(solution)/shard_map/all_to_all | solution.py:86
  548.4 150.6 %reduce-scatter.15.cloned.1.call-start = ((), (), s32[]{:S(2)}) async-start(), calls=%async_computation.23 | async-start | bytes 1179648 | tf_op jit(solution)/shard_map/reduce_scatter | solution.py:98
  553.9 145.1 %reduce-scatter.11.cloned.1.call-start = ((), (), s32[]{:S(2)}) async-start(), calls=%async_computation.21 | async-start | bytes 1179648 | tf_op jit(solution)/shard_map/reduce_scatter | solution.py:98
  600.3 25.7 %all-to-all-start.11 = ((f32[64,1,36]{2,1,0:T(1,128)}), f32[64,1,36]{2,1,0:T(1,128)}, u32[]{:S(2)}, u32[]{:S(2)}) async-start(f32[64,1,36]{2,1,0:T(1,128)} %copy.91), calls=%async_computation.17 | async-start | bytes 65536 | tf_op jit(solution)/shard_map/all_to_all | solution.py:89
  610.8 88.2 %reduce-scatter.9.cloned.1.call-start = ((), (), s32[]{:S(2)}) async-start(), calls=%async_computation.20 | async-start | bytes 1179648 | tf_op jit(solution)/shard_map/reduce_scatter | solution.py:98
  626.0 51.9 %all-to-all-start.10 = ((bf16[64,1,36,512]{3,2,1,0:T(8,128)(2,1)}), bf16[64,1,36,512]{3,2,1,0:T(8,128)(2,1)}, u32[]{:S(2)}, u32[]{:S(2)}) async-start(bf16[64,1,36,512]{3,2,1,0:T(8,128)(2,1)} %copy.86), calls=%async_computation.10 | async-start | bytes 5242880 | tf_op jit(solution)/shard_map/all_to_all | solution.py:89
  636.7 62.4 %reduce-scatter.7.cloned.1.call-start = ((), (), s32[]{:S(2)}) async-start(), calls=%async_computation.19 | async-start | bytes 1179648 | tf_op jit(solution)/shard_map/reduce_scatter | solution.py:98
  (23 other events, 146.3 us)
Sparse Core Ops, SparseCore 0:
  506.7 12.0 reduce-scatter.16
  521.8 12.1 reduce-scatter.12
  554.0 12.0 reduce-scatter.14
  599.0 12.0 reduce-scatter.10
  619.0 12.0 reduce-scatter.8
  646.3 12.0 reduce-scatter.6
where the time goes:
time: 716 us; the launch traced here: 706 us
  local copies, waits for them, and re-layouts  209 us (29%)
  waiting for transfers between devices  139 us (19%)
  starting transfers between devices  118 us (16%)
  matrix products  89.3 us (12%)
  other arithmetic  86.2 us (12%)
  blocking collectives  49.7 us (7%)
  between operations  15.3 us (2%)
    all_to_all x6, waiting for transfers between devices, exchange(): return lax.all_to_all(shaped, 'ep', 0, 0)  98.3 us
    all_to_all x6, starting transfers between devices, give_back(): returned = lax.all_to_all(expert_rows, 'ep', 0, 0)  58.8 us
    all_to_all x6, starting transfers between devices, exchange(): return lax.all_to_all(shaped, 'ep', 0, 0)  58.2 us
    all_to_all x1, blocking collectives, exchange(): return lax.all_to_all(shaped, 'ep', 0, 0)  49.7 us
    another operation x8, other arithmetic  41.6 us
    all_to_all x6, waiting for transfers between devices, give_back(): returned = lax.all_to_all(expert_rows, 'ep', 0, 0)  40.7 us
    gather x5, local copies, waits for them, and re-layouts, take_rows(): return jnp.take(values, row_tok, axis=0) * row_used[:, None]  36.9 us
    scatter x2, local copies, waits for them, and re-layouts, route_rows(): jnp.zeros((n_experts * capacity,), jnp.bfloat16).at[pair_row].set(1.0)  34.9 us
  transfers between devices with their start and end apart: 18, of which 8 were waited for; matrix products, arithmetic and copies ran while one was open for 40% of the time, Pallas kernels for 0%

commit v1 on v0

v1 whole, which is shorter than its diff:
```python
import functools

import jax
import jax.numpy as jnp
from jax import lax
from jax.experimental import pallas as pl
from jax.experimental.pallas import tpu as pltpu
from jax.sharding import PartitionSpec as P

F32, BF16, I32 = jnp.float32, jnp.bfloat16, jnp.int32
MAIN, REM = 32, 4
NN = (((1,), (0,)), ((), ()))
NT = (((1,), (1,)), ((), ()))
TN = (((0,), (0,)), ((), ()))


def mm(lhs, rhs, dims=NN):
    return lax.dot_general(lhs, rhs, dims, preferred_element_type=F32)


def iota(shape, dim):
    return lax.broadcasted_iota(I32, shape, dim)


def split3(value):
    high = value.astype(BF16)
    rest = value - high.astype(F32)
    mid = rest.astype(BF16)
    low = (rest - mid.astype(F32)).astype(BF16)
    return high, mid, low


def unpack_rem(tiles):
    steps = tiles.shape[0]
    pairs = steps // 2
    wide = tiles.astype(F32).reshape(pairs, 2, 2, 8, 128)
    even, odd = wide[:, 0], wide[:, 1]
    upper = iota((pairs, 8, 128), 1) < 4
    chunks = []
    for k in range(4):
        e, o = even[:, k // 2], odd[:, k // 2]
        picked = jnp.where(upper, e, pltpu.roll(o, 4, 1)) if k % 2 == 0 else jnp.where(upper, pltpu.roll(e, 4, 1), o)
        chunks.append(picked.reshape(pairs * 8, 128))
    return jnp.concatenate(chunks, axis=1).astype(BF16)


def pack_rem(rows):
    pairs = rows.shape[0] // 8
    c = [rows[:, 128 * k:128 * (k + 1)].reshape(pairs, 8, 128) for k in range(4)]
    upper = iota((pairs, 8, 128), 1) < 4
    even = [jnp.where(upper, c[2 * h], pltpu.roll(c[2 * h + 1], 4, 1)) for h in range(2)]
    odd = [jnp.where(upper, pltpu.roll(c[2 * h], 4, 1), c[2 * h + 1]) for h in range(2)]
    return jnp.stack([even[0], even[1], odd[0], odd[1]], axis=1).reshape(pairs * 2, 16, 128).astype(BF16)


class Exchange:
    def __init__(self, src, dst, sems, peers, size, count, back):
        self.src, self.dst, self.peers, self.size, self.count, self.back = src, dst, peers, size, count, back
        self.send_sems, self.recv_sems = sems

    def start(self, group):
        @pl.loop(0, self.size)
        def _(i):
            step = group * self.size + i

            @pl.when(step == 0)
            def _():
                for k, (src, dst) in enumerate(zip(self.src, self.dst)):
                    pltpu.make_async_copy(src.at[0], dst.at[0], self.recv_sems.at[k, 0]).start()

            @pl.when(step > 0)
            def _():
                peer = self.peers(step, self.back)
                for k, (src, dst) in enumerate(zip(self.src, self.dst)):
                    pltpu.make_async_remote_copy(
                        src_ref=src.at[step], dst_ref=dst.at[step], send_sem=self.send_sems.at[k, group],
                        recv_sem=self.recv_sems.at[k, group], device_id={'ep': peer},
                        device_id_type=pl.DeviceIdType.MESH).start()

    def wait_recv(self, group):
        for k, dst in enumerate(self.dst):
            part = dst.at[pl.ds(group * self.size, self.size)]
            pltpu.make_async_copy(part, part, self.recv_sems.at[k, group]).wait()

    def wait_sends(self):
        for group in range(self.count):
            first = 1 if group == 0 else 0
            for k, src in enumerate(self.src):
                part = src.at[pl.ds(group * self.size + first, self.size - first)]
                pltpu.make_async_copy(part, part, self.send_sems.at[k, group]).wait()


def moe_kernel(cfg, *refs):
    n_exp, base, groups, n_tok, top_k, dim, ffn = cfg
    size = n_exp // groups
    rows = size * (MAIN + REM)
    main_rows = size * MAIN
    (x_ref, dy_ref, route_a, route_b, gate_a, gate_b, w1_a, w3_a, w2_a, w1_b, w3_b, w2_b,
     xf_ref, gx_ref, dw1_a, dw3_a, dw2_a, dw1_b, dw3_b, dw2_b, dga_ref, dgb_ref,
     sa_m, sa_r, sb_m, sb_r, sc_m, sc_r, sd_m, sd_r, tx_m, tx_r, ty_m, ty_r, tz_m, tz_r,
     ra_m, ra_r, rb_m, rb_r, rdb_m, rdb_r, rda_m, rda_r,
     ga_s, ga_t, gb_s, gb_t, da_s, da_t, db_s, db_t,
     slot_a, slot_b, gt_a, gt_b, acc, x_mid, dy_mid, w13, w2, xc, hid, dact, gdy, dw13, dw2, in13, in2,
     send_sems, recv_sems, gsend_sems, grecv_sems, load_sems, dp_send, dp_recv, out_sems) = refs

    me = lax.axis_index('ep')
    dp = lax.axis_index('dp')
    stride = 21 if n_exp == 64 else 1

    def shift(step, back, origin):
        move = (stride * step) % n_exp
        digits = [(origin // (base * base), move // (base * base)), ((origin // base) % base, (move // base) % base),
                  (origin % base, move % base)]
        at = [((o - m + base) % base) if back else ((o + m) % base) for o, m in digits]
        return (at[0] * base + at[1]) * base + at[2]

    def peers(step, back):
        return shift(step, back, me)

    def exchange(index, src, dst, back):
        return Exchange(src, dst, (send_sems.at[index], recv_sems.at[index]), peers, size, groups, back)

    def small(index, src, dst, back):
        return Exchange((src,), (dst,), (gsend_sems.at[index], grecv_sems.at[index]), peers, size, groups, back)

    ex_xa = exchange(0, (sa_m, sa_r), (ra_m, ra_r), False)
    ex_oa = exchange(1, (sc_m, sc_r), (tx_m, tx_r), True)
    ex_xb = exchange(2, (sb_m, sb_r), (rb_m, rb_r), False)
    ex_ob = exchange(3, (sd_m, sd_r), (ty_m, ty_r), True)
    ex_dyb = exchange(4, (sa_m, sa_r), (rdb_m, rdb_r), False)
    ex_dub = exchange(5, (sc_m, sc_r), (tx_m, tx_r), True)
    ex_xa2 = exchange(6, (sb_m, sb_r), (ra_m, ra_r), False)
    ex_dya = exchange(7, (sa_m, sa_r), (rda_m, rda_r), False)
    ex_dua = exchange(8, (sd_m, sd_r), (tz_m, tz_r), True)
    ex_gb = small(0, gb_s, gb_t, False)
    ex_ga = small(1, ga_s, ga_t, False)
    ex_dgb = small(2, db_s, db_t, True)
    ex_dga = small(3, da_s, da_t, True)

    loads = []
    for k, (u1, u3, d2) in enumerate(((w1_a, w3_a, w2_a), (w1_b, w3_b, w2_b))):
        for j, (src, dst) in enumerate(((u1.at[0], w13.at[k, :, 0:ffn]), (u3.at[0], w13.at[k, :, ffn:2 * ffn]),
                                        (d2.at[0], w2.at[k]))):
            load = pltpu.make_async_copy(src, dst, load_sems.at[k, j])
            load.start()
            loads.append(load)

    def row_step(r):
        return jnp.where(r < main_rows, r // MAIN, (r - main_rows) // REM)

    def row_slot(r):
        return jnp.where(r < main_rows, r % MAIN, MAIN + (r - main_rows) % REM)

    def step_of_row():
        return (row_step(iota((rows, size), 0)) == iota((rows, size), 1)).astype(F32).astype(BF16)

    def row_of_step():
        return (row_step(iota((size, rows), 1)) == iota((size, rows), 0)).astype(F32).astype(BF16)

    def slot_lane():
        return row_slot(iota((rows, 128), 0)) == iota((rows, 128), 1)

    def make_plan(route_ref, gate_ref, slot_ref, gt_ref):
        owner = shift(iota((n_exp, n_tok), 0), False, me)
        hits = jnp.zeros((n_exp, n_tok), F32)
        gates = jnp.zeros((n_exp, n_tok), F32)
        for j in range(top_k):
            here = route_ref[j:j + 1, :] == owner
            hits = hits + here.astype(F32)
            gates = gates + jnp.where(here, gate_ref[j:j + 1, :], 0.0)
        before = (iota((n_tok, n_tok), 0) < iota((n_tok, n_tok), 1)).astype(F32).astype(BF16)
        earlier = mm(hits.astype(BF16), before)
        slot_ref[...] = jnp.where(hits > 0, earlier, 100.0)
        gt_ref[...] = gates

    def group_slice(ref, group):
        return ref[pl.ds(pl.multiple_of(group * size, size), size)]

    def pick_matrix(slot_ref, group):
        spread = mm(step_of_row(), group_slice(slot_ref, group).astype(BF16))
        want = row_slot(iota((rows, n_tok), 0)).astype(F32)
        return spread == want

    def put_mask(slot_ref, group):
        spread = mm(group_slice(slot_ref, group).astype(BF16), row_of_step(), TN)
        want = row_slot(iota((n_tok, rows), 1)).astype(F32)
        return spread == want

    def gate_matrix(slot_ref, gt_ref, group):
        mask = put_mask(slot_ref, group)
        back = row_of_step()
        parts = [jnp.where(mask, mm(part, back, TN), 0.0).astype(BF16) for part in split3(group_slice(gt_ref, group))]
        return jnp.concatenate(parts, axis=0)

    def store_block(main_ref, rem_ref, group, values):
        at = pl.ds(pl.multiple_of(group * size, size), size)
        main_ref[at] = values[:main_rows].astype(BF16).reshape(size, MAIN, dim)
        rem_ref[at] = pack_rem(values[main_rows:])

    def load_block(main_ref, rem_ref, group):
        main = group_slice(main_ref, group).reshape(main_rows, dim)
        return jnp.concatenate([main, unpack_rem(group_slice(rem_ref, group))], axis=0)

    def lanes_from_rows(column):
        spread = jnp.where(slot_lane(), jnp.broadcast_to(column, (rows, 128)), 0.0)
        back = row_of_step()
        high, mid, low = [mm(back, part) for part in split3(spread)]
        return (high + mid) + low

    def rows_from_lanes(lanes):
        back = step_of_row()
        high, mid, low = [mm(back, part) for part in split3(lanes)]
        return jnp.sum(jnp.where(slot_lane(), (high + mid) + low, 0.0), axis=1, keepdims=True)

    def store_small(ref, group, lanes):
        ref[pl.ds(pl.multiple_of(group * size, size), size)] = lanes.reshape(size, 1, 128)

    def load_small(ref, group):
        return group_slice(ref, group).reshape(size, 128)

    def fill(ex, slot_ref, source):
        @pl.loop(0, groups)
        def _(group):
            picked = pick_matrix(slot_ref, group).astype(F32).astype(BF16)
            store_block(ex.src[0], ex.src[1], group, mm(picked, source[...]))
            ex.start(group)

    def fill_gates(ex, slot_ref, gt_ref):
        @pl.loop(0, groups)
        def _(group):
            spread = jnp.zeros((rows, n_tok), F32)
            for part in split3(group_slice(gt_ref, group)):
                spread = spread + mm(step_of_row(), part)
            column = jnp.sum(jnp.where(pick_matrix(slot_ref, group), spread, 0.0), axis=1, keepdims=True)
            store_small(ex.src[0], group, lanes_from_rows(column))
            ex.start(group)

    def forward(layer, ex_in, ex_out):
        @pl.loop(0, groups)
        def _(group):
            ex_in.wait_recv(group)
            recv = load_block(ex_in.dst[0], ex_in.dst[1], group)
            pre = mm(recv, w13[layer])
            one, three = pre[:, :ffn], pre[:, ffn:]
            hidden = (one * jax.nn.sigmoid(one) * three).astype(BF16)
            store_block(ex_out.src[0], ex_out.src[1], group, mm(hidden, w2[layer]))
            ex_out.start(group)

    def mix_back(ex, slot_ref, gt_ref, base_ref, out_ref):
        acc[...] = base_ref[...].astype(F32)

        @pl.loop(0, groups)
        def _(group):
            weights = gate_matrix(slot_ref, gt_ref, group)
            ex.wait_recv(group)
            parts = mm(weights, load_block(ex.dst[0], ex.dst[1], group))
            acc[...] += (parts[:n_tok] + parts[n_tok:2 * n_tok]) + parts[2 * n_tok:]

        out_ref[...] = acc[...].astype(BF16)

    def add_back(ex, slot_ref, base_ref, out_ref):
        acc[...] = base_ref[...].astype(F32)

        @pl.loop(0, groups)
        def _(group):
            mask = put_mask(slot_ref, group).astype(F32).astype(BF16)
            ex.wait_recv(group)
            acc[...] += mm(mask, load_block(ex.dst[0], ex.dst[1], group))

        out_ref[...] = acc[...].astype(BF16)

    def backward(layer, recv_ex, ex_dy, ex_gate, ex_du, ex_dgate, wait_rows):
        @pl.loop(0, groups)
        def _(group):
            if wait_rows:
                recv_ex.wait_recv(group)
            at = pl.ds(pl.multiple_of(group * rows, rows), rows)
            recv = load_block(recv_ex.dst[0], recv_ex.dst[1], group)
            xc[at] = recv
            pre = mm(recv, w13[layer])
            one, three = pre[:, :ffn], pre[:, ffn:]
            sig = jax.nn.sigmoid(one)
            act = one * sig
            hidden = (act * three).astype(BF16)
            hid[at] = hidden
            ex_gate.wait_recv(group)
            gate = rows_from_lanes(load_small(ex_gate.dst[0], group))
            ex_dy.wait_recv(group)
            dyr = load_block(ex_dy.dst[0], ex_dy.dst[1], group)
            proj = mm(dyr, w2[layer], NT)
            gdy[at] = (gate * dyr.astype(F32)).astype(BF16)
            grad_h = gate * proj
            dact[at, 0:ffn] = (grad_h * three * sig * (1.0 + one * (1.0 - sig))).astype(BF16)
            dact[at, ffn:2 * ffn] = (grad_h * act).astype(BF16)
            store_block(ex_du.src[0], ex_du.src[1], group, mm(dact[at], w13[layer], NT))
            ex_du.start(group)
            store_small(ex_dgate.src[0], group,
                        lanes_from_rows(jnp.sum(proj * hidden.astype(F32), axis=1, keepdims=True)))
            ex_dgate.start(group)

    def partner_copy(src, dst, index):
        return pltpu.make_async_remote_copy(src_ref=src, dst_ref=dst, send_sem=dp_send.at[index],
                                            recv_sem=dp_recv.at[index], device_id={'dp': 1 - dp},
                                            device_id_type=pl.DeviceIdType.MESH)

    def half(count, which):
        return pl.ds(pl.multiple_of(which * (count // 2), 8), count // 2)

    def weight_grads(layer):
        dw13[layer] = jnp.zeros((dim, 2 * ffn), F32)
        dw2[layer] = jnp.zeros((ffn, dim), F32)

        @pl.loop(0, groups)
        def _(group):
            at = pl.ds(pl.multiple_of(group * rows, rows), rows)
            dw13[layer] += mm(xc[at], dact[at], TN)
            dw2[layer] += mm(hid[at], gdy[at], TN)

        sends = [partner_copy(dw13.at[layer, half(dim, 1 - dp)], in13.at[layer], 2 * layer),
                 partner_copy(dw2.at[layer, half(ffn, 1 - dp)], in2.at[layer], 2 * layer + 1)]
        for send in sends:
            send.start()
        return sends

    def finish_grads(layer, sends, out1, out3, out2):
        for send in sends:
            send.wait()
        in13[layer] += dw13[layer, half(dim, dp)]
        in2[layer] += dw2[layer, half(ffn, dp)]
        stores = [pltpu.make_async_copy(in13.at[layer, :, 0:ffn], out1.at[0], out_sems.at[layer, 0]),
                  pltpu.make_async_copy(in13.at[layer, :, ffn:2 * ffn], out3.at[0], out_sems.at[layer, 1]),
                  pltpu.make_async_copy(in2.at[layer], out2.at[0], out_sems.at[layer, 2])]
        for store in stores:
            store.start()
        return stores

    def gate_grads(ex, slot_ref, route_ref, out_ref):
        out_ref[...] = jnp.zeros(out_ref.shape, F32)

        @pl.loop(0, groups)
        def _(group):
            ex.wait_recv(group)
            column = rows_from_lanes(load_small(ex.dst[0], group))
            spread = jnp.where(pick_matrix(slot_ref, group), column, 0.0)
            high, mid, low = [mm(row_of_step(), part) for part in split3(spread)]
            per_step = (high + mid) + low
            owner = shift(iota((size, n_tok), 0) + group * size, False, me)
            for j in range(top_k):
                here = route_ref[j:j + 1, :] == owner
                out_ref[j:j + 1, :] += jnp.sum(jnp.where(here, per_step, 0.0), axis=0, keepdims=True)

    make_plan(route_a, gate_a, slot_a, gt_a)
    fill(ex_xa, slot_a, x_ref)
    make_plan(route_b, gate_b, slot_b, gt_b)
    for load in loads:
        load.wait()
    forward(0, ex_xa, ex_oa)
    mix_back(ex_oa, slot_a, gt_a, x_ref, x_mid)
    fill(ex_xb, slot_b, x_mid)
    forward(1, ex_xb, ex_ob)
    ex_xa.wait_sends()
    fill_gates(ex_gb, slot_b, gt_b)
    fill(ex_dyb, slot_b, dy_ref)
    ex_oa.wait_sends()
    backward(1, ex_xb, ex_dyb, ex_gb, ex_dub, ex_dgb, False)
    ex_xb.wait_sends()
    fill(ex_xa2, slot_a, x_ref)
    fill_gates(ex_ga, slot_a, gt_a)
    sends_b = weight_grads(1)
    ex_dyb.wait_sends()
    add_back(ex_dub, slot_b, dy_ref, dy_mid)
    fill(ex_dya, slot_a, dy_mid)
    mix_back(ex_ob, slot_b, gt_b, x_mid, xf_ref)
    stores_b = finish_grads(1, sends_b, dw1_b, dw3_b, dw2_b)
    gate_grads(ex_dgb, slot_b, route_b, dgb_ref)
    ex_ob.wait_sends()
    backward(0, ex_xa2, ex_dya, ex_ga, ex_dua, ex_dga, True)
    sends_a = weight_grads(0)
    stores_a = finish_grads(0, sends_a, dw1_a, dw3_a, dw2_a)
    add_back(ex_dua, slot_a, dy_mid, gx_ref)
    gate_grads(ex_dga, slot_a, route_a, dga_ref)
    for ex in (ex_dub, ex_xa2, ex_dya, ex_dua, ex_gb, ex_ga, ex_dgb, ex_dga):
        ex.wait_sends()
    for store in stores_b + stores_a:
        store.wait()


def solution(mesh):
    n_ep = mesh.shape['ep']
    base = round(n_ep ** (1 / 3))
    tok_spec = P(('pod', 'dp', 'ep'), None)
    weight_spec = P('ep', None, None)
    grad_spec = P(('pod', 'ep'), 'dp', None)
    groups = 4 if n_ep == 64 else 2

    def local_step(x_start, route_a, route_b, gate_a, gate_b, grad_out, w1_a, w3_a, w2_a, w1_b, w3_b, w2_b):
        n_tok, dim = x_start.shape
        top_k = route_a.shape[1]
        ffn = w1_a.shape[2]
        size = n_ep // groups
        rows = size * (MAIN + REM)
        cfg = (n_ep, base, groups, n_tok, top_k, dim, ffn)
        vmem = pl.BlockSpec(memory_space=pltpu.VMEM)
        any_space = pl.BlockSpec(memory_space=pl.ANY)
        block = [pltpu.VMEM((n_ep, MAIN, dim), BF16), pltpu.VMEM((n_ep, 16, 128), BF16)]
        lane = pltpu.VMEM((n_ep, 1, 128), F32)
        dma = pltpu.SemaphoreType.DMA
        scratch = block * 11 + [lane] * 8 + [pltpu.VMEM((n_ep, n_tok), F32)] * 4 + [
            pltpu.VMEM((n_tok, dim), F32),
            pltpu.VMEM((n_tok, dim), BF16),
            pltpu.VMEM((n_tok, dim), BF16),
            pltpu.VMEM((2, dim, 2 * ffn), BF16),
            pltpu.VMEM((2, ffn, dim), BF16),
            pltpu.VMEM((groups * rows, dim), BF16),
            pltpu.VMEM((groups * rows, ffn), BF16),
            pltpu.VMEM((groups * rows, 2 * ffn), BF16),
            pltpu.VMEM((groups * rows, dim), BF16),
            pltpu.VMEM((2, dim, 2 * ffn), F32),
            pltpu.VMEM((2, ffn, dim), F32),
            pltpu.VMEM((2, dim // 2, 2 * ffn), F32),
            pltpu.VMEM((2, ffn // 2, dim), F32),
            dma((9, 2, groups)), dma((9, 2, groups)), dma((4, 1, groups)), dma((4, 1, groups)),
            dma((2, 3)), dma((4,)), dma((4,)), dma((2, 3)),
        ]
        up = jax.ShapeDtypeStruct((1, dim // 2, ffn), F32)
        down = jax.ShapeDtypeStruct((1, ffn // 2, dim), F32)
        tok = jax.ShapeDtypeStruct((n_tok, dim), BF16)
        gate = jax.ShapeDtypeStruct((top_k, n_tok), F32)
        out = pl.pallas_call(
            functools.partial(moe_kernel, cfg),
            out_shape=(tok, tok, up, up, down, up, up, down, gate, gate),
            in_specs=[vmem] * 6 + [any_space] * 6,
            out_specs=(vmem, vmem) + (any_space,) * 6 + (vmem, vmem),
            scratch_shapes=scratch,
            compiler_params=pltpu.CompilerParams(has_side_effects=True, vmem_limit_bytes=63 * 1024 * 1024),
            name='moe_step',
        )(x_start, grad_out, route_a.T, route_b.T, gate_a.T, gate_b.T, w1_a, w3_a, w2_a, w1_b, w3_b, w2_b)
        return out[:8] + (out[8].T, out[9].T)

    return jax.shard_map(local_step, mesh=mesh,
                         in_specs=(tok_spec,) * 6 + (weight_spec,) * 6,
                         out_specs=(tok_spec, tok_spec) + (grad_spec,) * 6 + (tok_spec, tok_spec),
                         check_vma=False)
```

time: 716 us -> 352 us (0.49)
  Pallas kernels: 0 us -> 338 us
  local copies, waits for them, and re-layouts: 209 us -> 10.2 us
  waiting for transfers between devices: 139 us -> 0 us
  starting transfers between devices: 118 us -> 0 us
  matrix products: 89.3 us -> 0 us
  other arithmetic: 86.2 us -> 0 us
  blocking collectives: 49.7 us -> 0 us
  between operations: 15.3 us -> 0.68 us
    pallas_call x0 -> x1, Pallas kernels: none -> 338 us  [local_step(): pl.pallas_call(functools.partial(moe_kernel, cfg), out_shape=(tok, tok, u...]
    all_to_all x12 -> x0, waiting for transfers between devices: 139 us -> none  [the longest x6 98.3 us: exchange(): return lax.all_to_all(shaped, 'ep', 0, 0)]
    all_to_all x12 -> x0, starting transfers between devices: 117 us -> none  [the longest x6 58.8 us: give_back(): returned = lax.all_to_all(expert_rows, 'ep', 0, 0)]
    dot_general x20 -> x0, matrix products: 89.3 us -> none  [the longest x2 15.9 us: expert_backward(): jnp.einsum('secd,efd->escf', recv_dy, w_down, preferred_element_type=jnp....]
    gather x11 -> x0, local copies, waits for them, and re-layouts: 75.3 us -> none  [the longest x5 36.9 us: take_rows(): return jnp.take(values, row_tok, axis=0) * row_used[:, None]]
    scatter x6 -> x0, local copies, waits for them, and re-layouts: 59.9 us -> none  [the longest x2 34.9 us: route_rows(): jnp.zeros((n_experts * capacity,), jnp.bfloat16).at[pair_row].set(1.0)]
    all_to_all x1 -> x0, blocking collectives: 49.7 us -> none  [exchange(): return lax.all_to_all(shaped, 'ep', 0, 0)]
    another operation x8 -> x0, other arithmetic: 41.6 us -> none
  transfers between devices with their start and end apart: 18 -> 0, of which waited for: 8 -> 0; matrix products, arithmetic and copies ran while one was open for 40% -> 0% of each run, Pallas kernels for 0% -> 0%
where the time goes in v1:
time: 352 us; the launch traced here: 349 us
  Pallas kernels  338 us (96%)
  local copies, waits for them, and re-layouts  10.2 us (3%)
    pallas_call x1, Pallas kernels, local_step(): pl.pallas_call(functools.partial(moe_kernel, cfg), out_shape=(tok, tok, u...  338 us
    unnamed x28, local copies, waits for them, and re-layouts  10.2 us

profile of v1, /device:TPU:2, one launch (start us, length us, event | category | flops | bytes accessed | tf_op | source)
XLA Modules:
  0.0 348.9 jit_solution(9762777262373949927)
XLA Ops:
  0.6 338.0 %moe_step.1 = (bf16[256,512]{1,0:T(8,128)(2,1)}, bf16[256,512]{1,0:T(8,128)(2,1)}, f32[1,256,384]{2,1,0:T(8,128)}, f32[1,256,384]{2,1,0:T(8,128)}, f32[1,192,512...) custom-call(bf16[256,512]{1,0:T(8,128)(2,1)} %refs_0_.1, ...), custom_call_target="tpu_custom_call" | custom-call | tf_op jit(solution)/shard_map/moe_step/pallas_call | solution.py:429
  338.6 0.0 copy-start.6
  338.7 0.0 copy-start.5
  338.7 1.7 copy.32
  340.4 0.0 copy-done.6
  340.4 0.7 copy.33
  341.1 0.0 copy-done.5
  341.1 0.0 copy-start.4
  341.1 0.7 copy.34
  341.9 0.4 copy-done.4
  342.2 0.0 copy-start.3
  342.2 0.7 copy.35
  343.0 0.4 copy-done.3
  343.4 0.0 copy-start.2
  343.4 0.7 copy.36
  344.1 0.4 copy-done.2
  344.5 0.0 copy-start.1
  344.5 0.7 copy.37
  345.3 0.4 copy-done.1
  345.7 0.0 copy-start
  345.7 0.7 copy.38
  346.4 0.4 copy-done
  346.8 0.0 copy-start.8
  346.8 0.7 copy.39
  347.5 0.0 copy-done.8
  347.5 0.0 copy-start.7
  347.6 0.6 copy.40
  348.2 0.1 copy-done.7
  348.3 0.6 copy.41
Async XLA Ops:
  338.6 1.8 copy-start.6
  338.7 2.5 copy-start.5
  341.1 1.1 copy-start.4
  342.2 1.1 copy-start.3
  343.4 1.1 copy-start.2
  344.5 1.1 copy-start.1
  345.7 1.1 copy-start
  346.8 0.8 copy-start.8
  347.5 0.7 copy-start.7

commit v2 on v1

--- a/solution.py
+++ b/solution.py
@@ -9,6 +9,7 @@
 
 F32, BF16, I32 = jnp.float32, jnp.bfloat16, jnp.int32
 MAIN, REM = 32, 4
+NAMES = ('xa', 'oa', 'xb', 'ob', 'dyb', 'dub', 'xa2', 'dya', 'dua', 'gb', 'ga', 'dgb', 'dga')
 NN = (((1,), (0,)), ((), ()))
 NT = (((1,), (1,)), ((), ()))
 TN = (((0,), (0,)), ((), ()))
@@ -54,7 +55,8 @@
 
 
 class Exchange:
-    def __init__(self, src, dst, sems, peers, size, count, back):
+    def __init__(self, name, src, dst, sems, peers, size, count, back):
+        self.name = name
         self.src, self.dst, self.peers, self.size, self.count, self.back = src, dst, peers, size, count, back
         self.send_sems, self.recv_sems = sems
 
@@ -65,29 +67,26 @@
 
             @pl.when(step == 0)
             def _():
-                for k, (src, dst) in enumerate(zip(self.src, self.dst)):
-                    pltpu.make_async_copy(src.at[0], dst.at[0], self.recv_sems.at[k, 0]).start()
+                pltpu.make_async_copy(self.src.at[0], self.dst.at[0], self.recv_sems.at[0]).start()
 
             @pl.when(step > 0)
             def _():
-                peer = self.peers(step, self.back)
-                for k, (src, dst) in enumerate(zip(self.src, self.dst)):
-                    pltpu.make_async_remote_copy(
-                        src_ref=src.at[step], dst_ref=dst.at[step], send_sem=self.send_sems.at[k, group],
-                        recv_sem=self.recv_sems.at[k, group], device_id={'ep': peer},
-                        device_id_type=pl.DeviceIdType.MESH).start()
+                pltpu.make_async_remote_copy(
+                    src_ref=self.src.at[step], dst_ref=self.dst.at[step], send_sem=self.send_sems.at[group],
+                    recv_sem=self.recv_sems.at[group], device_id={'ep': self.peers(step, self.back)},
+                    device_id_type=pl.DeviceIdType.MESH).start()
 
     def wait_recv(self, group):
-        for k, dst in enumerate(self.dst):
-            part = dst.at[pl.ds(group * self.size, self.size)]
-            pltpu.make_async_copy(part, part, self.recv_sems.at[k, group]).wait()
+        with jax.named_scope('recv_' + self.name):
+            part = self.dst.at[pl.ds(group * self.size, self.size)]
+            pltpu.make_async_copy(part, part, self.recv_sems.at[group]).wait()
 
     def wait_sends(self):
-        for group in range(self.count):
-            first = 1 if group == 0 else 0
-            for k, src in enumerate(self.src):
-                part = src.at[pl.ds(group * self.size + first, self.size - first)]
-                pltpu.make_async_copy(part, part, self.send_sems.at[k, group]).wait()
+        with jax.named_scope('sent_' + self.name):
+            for group in range(self.count):
+                first = 1 if group == 0 else 0
+                part = self.src.at[pl.ds(group * self.size + first, self.size - first)]
+                pltpu.make_async_copy(part, part, self.send_sems.at[group]).wait()
 
 
 def moe_kernel(cfg, *refs):
@@ -97,20 +96,18 @@
     main_rows = size * MAIN
     (x_ref, dy_ref, route_a, route_b, gate_a, gate_b, w1_a, w3_a, w2_a, w1_b, w3_b, w2_b,
      xf_ref, gx_ref, dw1_a, dw3_a, dw2_a, dw1_b, dw3_b, dw2_b, dga_ref, dgb_ref,
-     sa_m, sa_r, sb_m, sb_r, sc_m, sc_r, sd_m, sd_r, tx_m, tx_r, ty_m, ty_r, tz_m, tz_r,
-     ra_m, ra_r, rb_m, rb_r, rdb_m, rdb_r, rda_m, rda_r,
+     sa, sb, sc, sd, tx, ty, tz, ra, rb, rdb, rda,
      ga_s, ga_t, gb_s, gb_t, da_s, da_t, db_s, db_t,
      slot_a, slot_b, gt_a, gt_b, acc, x_mid, dy_mid, w13, w2, xc, hid, dact, gdy, dw13, dw2, in13, in2,
      send_sems, recv_sems, gsend_sems, grecv_sems, load_sems, dp_send, dp_recv, out_sems) = refs
 
     me = lax.axis_index('ep')
     dp = lax.axis_index('dp')
-    stride = 21 if n_exp == 64 else 1
 
     def shift(step, back, origin):
-        move = (stride * step) % n_exp
-        digits = [(origin // (base * base), move // (base * base)), ((origin // base) % base, (move // base) % base),
-                  (origin % base, move % base)]
+        turn, other = step // 2, (step % 2) * (base // 2)
+        moves = ((turn // (base * base) + other) % base, ((turn // base) % base + other) % base, (turn % base + other) % base)
+        digits = [(origin // (base * base), moves[0]), ((origin // base) % base, moves[1]), (origin % base, moves[2])]
         at = [((o - m + base) % base) if back else ((o + m) % base) for o, m in digits]
         return (at[0] * base + at[1]) * base + at[2]
 
@@ -118,24 +115,32 @@
         return shift(step, back, me)
 
     def exchange(index, src, dst, back):
-        return Exchange(src, dst, (send_sems.at[index], recv_sems.at[index]), peers, size, groups, back)
+        return Exchange(NAMES[index], src, dst, (send_sems.at[index], recv_sems.at[index]), peers, size, groups, back)
 
     def small(index, src, dst, back):
-        return Exchange((src,), (dst,), (gsend_sems.at[index], grecv_sems.at[index]), peers, size, groups, back)
-
-    ex_xa = exchange(0, (sa_m, sa_r), (ra_m, ra_r), False)
-    ex_oa = exchange(1, (sc_m, sc_r), (tx_m, tx_r), True)
-    ex_xb = exchange(2, (sb_m, sb_r), (rb_m, rb_r), False)
-    ex_ob = exchange(3, (sd_m, sd_r), (ty_m, ty_r), True)
-    ex_dyb = exchange(4, (sa_m, sa_r), (rdb_m, rdb_r), False)
-    ex_dub = exchange(5, (sc_m, sc_r), (tx_m, tx_r), True)
-    ex_xa2 = exchange(6, (sb_m, sb_r), (ra_m, ra_r), False)
-    ex_dya = exchange(7, (sa_m, sa_r), (rda_m, rda_r), False)
-    ex_dua = exchange(8, (sd_m, sd_r), (tz_m, tz_r), True)
+        return Exchange(NAMES[9 + index], src, dst, (gsend_sems.at[index], grecv_sems.at[index]), peers, size, groups, back)
+
+    ex_xa = exchange(0, sa, ra, False)
+    ex_oa = exchange(1, sc, tx, True)
+    ex_xb = exchange(2, sb, rb, False)
+    ex_ob = exchange(3, sd, ty, True)
+    ex_dyb = exchange(4, sa, rdb, False)
+    ex_dub = exchange(5, sc, tx, True)
+    ex_xa2 = exchange(6, sb, ra, False)
+    ex_dya = exchange(7, sa, rda, False)
+    ex_dua = exchange(8, sd, tz, True)
     ex_gb = small(0, gb_s, gb_t, False)
     ex_ga = small(1, ga_s, ga_t, False)
     ex_dgb = small(2, db_s, db_t, True)
     ex_dga = small(3, da_s, da_t, True)
+
+    barrier = pltpu.get_barrier_semaphore()
+
+    @pl.loop(1, n_exp)
+    def _(step):
+        pl.semaphore_signal(barrier, inc=1, device_id={'ep': peers(step, False)}, device_id_type=pl.DeviceIdType.MESH)
+
+    pl.semaphore_signal(barrier, inc=1, device_id={'dp': 1 - dp}, device_id_type=pl.DeviceIdType.MESH)
 
     loads = []
     for k, (u1, u3, d2) in enumerate(((w1_a, w3_a, w2_a), (w1_b, w3_b, w2_b))):
@@ -192,14 +197,17 @@
         parts = [jnp.where(mask, mm(part, back, TN), 0.0).astype(BF16) for part in split3(group_slice(gt_ref, group))]
         return jnp.concatenate(parts, axis=0)
 
-    def store_block(main_ref, rem_ref, group, values):
+    def store_block(ref, group, values):
         at = pl.ds(pl.multiple_of(group * size, size), size)
-        main_ref[at] = values[:main_rows].astype(BF16).reshape(size, MAIN, dim)
-        rem_ref[at] = pack_rem(values[main_rows:])
-
-    def load_block(main_ref, rem_ref, group):
-        main = group_slice(main_ref, group).reshape(main_rows, dim)
-        return jnp.concatenate([main, unpack_rem(group_slice(rem_ref, group))], axis=0)
+        main = values[:main_rows].astype(BF16)
+        for k in range(4):
+            ref[at, MAIN * k:MAIN * (k + 1), :] = main[:, 128 * k:128 * (k + 1)].reshape(size, MAIN, 128)
+        ref[at, 4 * MAIN:4 * MAIN + 16, :] = pack_rem(values[main_rows:])
+
+    def load_block(ref, group):
+        at = pl.ds(pl.multiple_of(group * size, size), size)
+        main = jnp.concatenate([ref[at, MAIN * k:MAIN * (k + 1), :].reshape(main_rows, 128) for k in range(4)], axis=1)
+        return jnp.concatenate([main, unpack_rem(ref[at, 4 * MAIN:4 * MAIN + 16, :])], axis=0)
 
     def lanes_from_rows(column):
         spread = jnp.where(slot_lane(), jnp.broadcast_to(column, (rows, 128)), 0.0)
@@ -218,12 +226,13 @@
     def load_small(ref, group):
         return group_slice(ref, group).reshape(size, 128)
 
-    def fill(ex, slot_ref, source):
+    def fill(ex, slot_ref, source, send=True):
         @pl.loop(0, groups)
         def _(group):
             picked = pick_matrix(slot_ref, group).astype(F32).astype(BF16)
-            store_block(ex.src[0], ex.src[1], group, mm(picked, source[...]))
-            ex.start(group)
+            store_block(ex.src, group, mm(picked, source[...]))
+            if send:
+                ex.start(group)
 
     def fill_gates(ex, slot_ref, gt_ref):
         @pl.loop(0, groups)
@@ -232,18 +241,18 @@
             for part in split3(group_slice(gt_ref, group)):
                 spread = spread + mm(step_of_row(), part)
             column = jnp.sum(jnp.where(pick_matrix(slot_ref, group), spread, 0.0), axis=1, keepdims=True)
-            store_small(ex.src[0], group, lanes_from_rows(column))
+            store_small(ex.src, group, lanes_from_rows(column))
             ex.start(group)
 
     def forward(layer, ex_in, ex_out):
         @pl.loop(0, groups)
         def _(group):
             ex_in.wait_recv(group)
-            recv = load_block(ex_in.dst[0], ex_in.dst[1], group)
+            recv = load_block(ex_in.dst, group)
             pre = mm(recv, w13[layer])
             one, three = pre[:, :ffn], pre[:, ffn:]
             hidden = (one * jax.nn.sigmoid(one) * three).astype(BF16)
-            store_block(ex_out.src[0], ex_out.src[1], group, mm(hidden, w2[layer]))
+            store_block(ex_out.src, group, mm(hidden, w2[layer]))
             ex_out.start(group)
 
     def mix_back(ex, slot_ref, gt_ref, base_ref, out_ref):
@@ -253,7 +262,7 @@
         def _(group):
             weights = gate_matrix(slot_ref, gt_ref, group)
             ex.wait_recv(group)
-            parts = mm(weights, load_block(ex.dst[0], ex.dst[1], group))
+            parts = mm(weights, load_block(ex.dst, group))
             acc[...] += (parts[:n_tok] + parts[n_tok:2 * n_tok]) + parts[2 * n_tok:]
 
         out_ref[...] = acc[...].astype(BF16)
@@ -265,7 +274,7 @@
         def _(group):
             mask = put_mask(slot_ref, group).astype(F32).astype(BF16)
             ex.wait_recv(group)
-            acc[...] += mm(mask, load_block(ex.dst[0], ex.dst[1], group))
+            acc[...] += mm(mask, load_block(ex.dst, group))
 
         out_ref[...] = acc[...].astype(BF16)
 
@@ -275,7 +284,7 @@
             if wait_rows:
                 recv_ex.wait_recv(group)
             at = pl.ds(pl.multiple_of(group * rows, rows), rows)
-            recv = load_block(recv_ex.dst[0], recv_ex.dst[1], group)
+            recv = load_block(recv_ex.dst, group)
             xc[at] = recv
             pre = mm(recv, w13[layer])
             one, three = pre[:, :ffn], pre[:, ffn:]
@@ -284,17 +293,17 @@
             hidden = (act * three).astype(BF16)
             hid[at] = hidden
             ex_gate.wait_recv(group)
-            gate = rows_from_lanes(load_small(ex_gate.dst[0], group))
+            gate = rows_from_lanes(load_small(ex_gate.dst, group))
             ex_dy.wait_recv(group)
-            dyr = load_block(ex_dy.dst[0], ex_dy.dst[1], group)
+            dyr = load_block(ex_dy.dst, group)
             proj = mm(dyr, w2[layer], NT)
             gdy[at] = (gate * dyr.astype(F32)).astype(BF16)
             grad_h = gate * proj
             dact[at, 0:ffn] = (grad_h * three * sig * (1.0 + one * (1.0 - sig))).astype(BF16)
             dact[at, ffn:2 * ffn] = (grad_h * act).astype(BF16)
-            store_block(ex_du.src[0], ex_du.src[1], group, mm(dact[at], w13[layer], NT))
+            store_block(ex_du.src, group, mm(dact[at], w13[layer], NT))
             ex_du.start(group)
-            store_small(ex_dgate.src[0], group,
+            store_small(ex_dgate.src, group,
                         lanes_from_rows(jnp.sum(proj * hidden.astype(F32), axis=1, keepdims=True)))
             ex_dgate.start(group)
 
@@ -340,7 +349,7 @@
         @pl.loop(0, groups)
         def _(group):
             ex.wait_recv(group)
-            column = rows_from_lanes(load_small(ex.dst[0], group))
+            column = rows_from_lanes(load_small(ex.dst, group))
             spread = jnp.where(pick_matrix(slot_ref, group), column, 0.0)
             high, mid, low = [mm(row_of_step(), part) for part in split3(spread)]
             per_step = (high + mid) + low
@@ -349,40 +358,86 @@
                 here = route_ref[j:j + 1, :] == owner
                 out_ref[j:j + 1, :] += jnp.sum(jnp.where(here, per_step, 0.0), axis=0, keepdims=True)
 
-    make_plan(route_a, gate_a, slot_a, gt_a)
-    fill(ex_xa, slot_a, x_ref)
-    make_plan(route_b, gate_b, slot_b, gt_b)
+    with jax.named_scope('make_plan_a'):
+        make_plan(route_a, gate_a, slot_a, gt_a)
+    with jax.named_scope('fill_xa'):
+        fill(ex_xa, slot_a, x_ref, send=False)
+    with jax.named_scope('entry'):
+        pl.semaphore_wait(barrier, n_exp)
+
+    @pl.loop(0, groups)
+    def _(group):
+        ex_xa.start(group)
+
+    with jax.named_scope('make_plan_b'):
+        make_plan(route_b, gate_b, slot_b, gt_b)
     for load in loads:
         load.wait()
-    forward(0, ex_xa, ex_oa)
-    mix_back(ex_oa, slot_a, gt_a, x_ref, x_mid)
-    fill(ex_xb, slot_b, x_mid)
-    forward(1, ex_xb, ex_ob)
+    with jax.named_scope('forward_l0'):
+        forward(0, ex_xa, ex_oa)
+    with jax.named_scope('mix_back_oa'):
+        mix_back(ex_oa, slot_a, gt_a, x_ref, x_mid)
+    with jax.named_scope('fill_xb'):
+        fill(ex_xb, slot_b, x_mid)
+    with jax.named_scope('forward_l1'):
+        forward(1, ex_xb, ex_ob)
     ex_xa.wait_sends()
-    fill_gates(ex_gb, slot_b, gt_b)
-    fill(ex_dyb, slot_b, dy_ref)
+    with jax.named_scope('fill_gates_gb'):
+        fill_gates(ex_gb, slot_b, gt_b)
+    with jax.named_scope('fill_dyb'):
+        fill(ex_dyb, slot_b, dy_ref)
     ex_oa.wait_sends()
-    backward(1, ex_xb, ex_dyb, ex_gb, ex_dub, ex_dgb, False)
+    with jax.named_scope('backward_l1'):
+        backward(1, ex_xb, ex_dyb, ex_gb, ex_dub, ex_dgb, False)
     ex_xb.wait_sends()
-    fill(ex_xa2, slot_a, x_ref)
-    fill_gates(ex_ga, slot_a, gt_a)
-    sends_b = weight_grads(1)
+    with jax.named_scope('fill_xa2'):
+        fill(ex_xa2, slot_a, x_ref)
+    with jax.named_scope('fill_gates_ga'):
+        fill_gates(ex_ga, slot_a, gt_a)
+    with jax.named_scope('weight_grads_l1'):
+        sends_b = weight_grads(1)
     ex_dyb.wait_sends()
-    add_back(ex_dub, slot_b, dy_ref, dy_mid)
-    fill(ex_dya, slot_a, dy_mid)
-    mix_back(ex_ob, slot_b, gt_b, x_mid, xf_ref)
-    stores_b = finish_grads(1, sends_b, dw1_b, dw3_b, dw2_b)
-    gate_grads(ex_dgb, slot_b, route_b, dgb_ref)
+    with jax.named_scope('add_back_dub'):
+        add_back(ex_dub, slot_b, dy_ref, dy_mid)
+    with jax.named_scope('fill_dya'):
+        fill(ex_dya, slot_a, dy_mid)
+    with jax.named_scope('mix_back_ob'):
+        mix_back(ex_ob, slot_b, gt_b, x_mid, xf_ref)
+    with jax.named_scope('finish_grads_l1'):
+        stores_b = finish_grads(1, sends_b, dw1_b, dw3_b, dw2_b)
+    with jax.named_scope('gate_grads_dgb'):
+        gate_grads(ex_dgb, slot_b, route_b, dgb_ref)
     ex_ob.wait_sends()
-    backward(0, ex_xa2, ex_dya, ex_ga, ex_dua, ex_dga, True)
-    sends_a = weight_grads(0)
-    stores_a = finish_grads(0, sends_a, dw1_a, dw3_a, dw2_a)
-    add_back(ex_dua, slot_a, dy_mid, gx_ref)
-    gate_grads(ex_dga, slot_a, route_a, dga_ref)
+    with jax.named_scope('backward_l0'):
+        backward(0, ex_xa2, ex_dya, ex_ga, ex_dua, ex_dga, True)
+    with jax.named_scope('weight_grads_l0'):
+        sends_a = weight_grads(0)
+    with jax.named_scope('finish_grads_l0'):
+        stores_a = finish_grads(0, sends_a, dw1_a, dw3_a, dw2_a)
+    with jax.named_scope('add_back_dua'):
+        add_back(ex_dua, slot_a, dy_mid, gx_ref)
+    with jax.named_scope('gate_grads_dga'):
+        gate_grads(ex_dga, slot_a, route_a, dga_ref)
     for ex in (ex_dub, ex_xa2, ex_dya, ex_dua, ex_gb, ex_ga, ex_dgb, ex_dga):
         ex.wait_sends()
     for store in stores_b + stores_a:
         store.wait()
+
+
+def write_kernel(*refs):
+    sources, results, buffers, sems = refs[:10], refs[10:20], refs[20:28], refs[28]
+    reads = [pltpu.make_async_copy(sources[k], buffers[k], sems.at[0, k]) for k in range(8)]
+    writes = [pltpu.make_async_copy(buffers[k], results[k], sems.at[1, k]) for k in range(8)]
+    for read in reads:
+        read.start()
+    for k in (8, 9):
+        top_k = results[k].shape[1]
+        results[k][...] = sources[k][...].T[:, :top_k]
+    for read, write in zip(reads, writes):
+        read.wait()
+        write.start()
+    for write in writes:
+        write.wait()
 
 
 def solution(mesh):
@@ -402,7 +457,7 @@
         cfg = (n_ep, base, groups, n_tok, top_k, dim, ffn)
         vmem = pl.BlockSpec(memory_space=pltpu.VMEM)
         any_space = pl.BlockSpec(memory_space=pl.ANY)
-        block = [pltpu.VMEM((n_ep, MAIN, dim), BF16), pltpu.VMEM((n_ep, 16, 128), BF16)]
+        block = [pltpu.VMEM((n_ep, 4 * MAIN + 16, 128), BF16)]
         lane = pltpu.VMEM((n_ep, 1, 128), F32)
         dma = pltpu.SemaphoreType.DMA
         scratch = block * 11 + [lane] * 8 + [pltpu.VMEM((n_ep, n_tok), F32)] * 4 + [
@@ -419,23 +474,32 @@
             pltpu.VMEM((2, ffn, dim), F32),
             pltpu.VMEM((2, dim // 2, 2 * ffn), F32),
             pltpu.VMEM((2, ffn // 2, dim), F32),
-            dma((9, 2, groups)), dma((9, 2, groups)), dma((4, 1, groups)), dma((4, 1, groups)),
+            dma((9, groups)), dma((9, groups)), dma((4, groups)), dma((4, groups)),
             dma((2, 3)), dma((4,)), dma((4,)), dma((2, 3)),
         ]
         up = jax.ShapeDtypeStruct((1, dim // 2, ffn), F32)
         down = jax.ShapeDtypeStruct((1, ffn // 2, dim), F32)
         tok = jax.ShapeDtypeStruct((n_tok, dim), BF16)
-        gate = jax.ShapeDtypeStruct((top_k, n_tok), F32)
+        gate = jax.ShapeDtypeStruct((8, n_tok), F32)
         out = pl.pallas_call(
             functools.partial(moe_kernel, cfg),
             out_shape=(tok, tok, up, up, down, up, up, down, gate, gate),
             in_specs=[vmem] * 6 + [any_space] * 6,
             out_specs=(vmem, vmem) + (any_space,) * 6 + (vmem, vmem),
             scratch_shapes=scratch,
-            compiler_params=pltpu.CompilerParams(has_side_effects=True, vmem_limit_bytes=63 * 1024 * 1024),
+            compiler_params=pltpu.CompilerParams(has_side_effects=True, collective_id=0, vmem_limit_bytes=63 * 1024 * 1024),
             name='moe_step',
         )(x_start, grad_out, route_a.T, route_b.T, gate_a.T, gate_b.T, w1_a, w3_a, w2_a, w1_b, w3_b, w2_b)
-        return out[:8] + (out[8].T, out[9].T)
+        shapes = [jax.ShapeDtypeStruct(o.shape, o.dtype) for o in out[:8]]
+        pair = jax.ShapeDtypeStruct((n_tok, top_k), F32)
+        return pl.pallas_call(
+            write_kernel,
+            out_shape=tuple(shapes) + (pair, pair),
+            in_specs=[any_space] * 8 + [vmem] * 2,
+            out_specs=(any_space,) * 8 + (vmem, vmem),
+            scratch_shapes=[pltpu.VMEM(o.shape, o.dtype) for o in out[:8]] + [dma((2, 8))],
+            name='write_out',
+        )(*out)
 
     return jax.shard_map(local_step, mesh=mesh,
                          in_specs=(tok_spec,) * 6 + (weight_spec,) * 6,

time: 352 us -> 346 us (0.983)
  local copies, waits for them, and re-layouts: 10.2 us -> 2.3 us
    unnamed x28 -> x2, local copies, waits for them, and re-layouts: 10.2 us -> 0.01 us
    pallas_call x0 -> x1, Pallas kernels: none -> 4.13 us  [local_step(): pl.pallas_call(write_kernel, out_shape=tuple(shapes) + (pair, pair), in_s...]
where the time goes in v2:
time: 346 us; the launch traced here: 343 us
  Pallas kernels  340 us (98%)
    pallas_call x1, Pallas kernels, local_step(): pl.pallas_call(functools.partial(moe_kernel, cfg), out_shape=(tok, tok, u...  336 us

profile of v2, /device:TPU:2, one launch (start us, length us, event | category | flops | bytes accessed | tf_op | source)
XLA Modules:
  0.0 343.3 jit_solution(15479380864928589591)
XLA Ops:
  0.6 336.2 %moe_step.1 = (bf16[256,512]{1,0:T(8,128)(2,1)}, bf16[256,512]{1,0:T(8,128)(2,1)}, f32[1,256,384]{2,1,0:T(8,128)}, f32[1,256,384]{2,1,0:T(8,128)}, f32[1,192,512...) custom-call(bf16[256,512]{1,0:T(8,128)(2,1)} %refs_0_.1, ...), custom_call_target="tpu_custom_call" | custom-call | tf_op jit(solution)/shard_map/moe_step/pallas_call | solution.py:484
  336.8 4.1 %write_out.1 = (bf16[256,512]{1,0:T(8,128)(2,1)}, bf16[256,512]{1,0:T(8,128)(2,1)}, f32[1,256,384]{2,1,0:T(8,128)}, f32[1,256,384]{2,1,0:T(8,128)}, f32[1,192,51...) custom-call(bf16[256,512]{1,0:T(8,128)(2,1)} %get-tuple-element.20.r, ...), custom_call_target="tpu_custom_call" | custom-call | tf_op jit(solution)/shard_map/write_out/pallas_call | solution.py:495
  341.0 0.0 copy-start
  341.0 1.6 copy.22
  342.6 0.0 copy-done
  342.6 0.7 copy.23
Async XLA Ops:
  341.0 1.6 copy-start

commit v3 on v2

--- a/solution.py
+++ b/solution.py
@@ -98,7 +98,7 @@
      xf_ref, gx_ref, dw1_a, dw3_a, dw2_a, dw1_b, dw3_b, dw2_b, dga_ref, dgb_ref,
      sa, sb, sc, sd, tx, ty, tz, ra, rb, rdb, rda,
      ga_s, ga_t, gb_s, gb_t, da_s, da_t, db_s, db_t,
-     slot_a, slot_b, gt_a, gt_b, acc, x_mid, dy_mid, w13, w2, xc, hid, dact, gdy, dw13, dw2, in13, in2,
+     slot_a, slot_b, gt_a, gt_b, acc, x_mid, dy_mid, w13, w2, xc, hid, pre_act, dact, gdy, dw13, dw2, in13, in2,
      send_sems, recv_sems, gsend_sems, grecv_sems, load_sems, dp_send, dp_recv, out_sems) = refs
 
     me = lax.axis_index('ep')
@@ -267,7 +267,7 @@
 
         out_ref[...] = acc[...].astype(BF16)
 
-    def add_back(ex, slot_ref, base_ref, out_ref):
+    def add_back(ex, slot_ref, base_ref, out_ref, beside=None):
         acc[...] = base_ref[...].astype(F32)
 
         @pl.loop(0, groups)
@@ -275,10 +275,12 @@
             mask = put_mask(slot_ref, group).astype(F32).astype(BF16)
             ex.wait_recv(group)
             acc[...] += mm(mask, load_block(ex.dst, group))
+            if beside is not None:
+                beside(group)
 
         out_ref[...] = acc[...].astype(BF16)
 
-    def backward(layer, recv_ex, ex_dy, ex_gate, ex_du, ex_dgate, wait_rows):
+    def recompute(layer, recv_ex, wait_rows):
         @pl.loop(0, groups)
         def _(group):
             if wait_rows:
@@ -287,24 +289,29 @@
             recv = load_block(recv_ex.dst, group)
             xc[at] = recv
             pre = mm(recv, w13[layer])
+            pre_act[at] = pre
             one, three = pre[:, :ffn], pre[:, ffn:]
-            sig = jax.nn.sigmoid(one)
-            act = one * sig
-            hidden = (act * three).astype(BF16)
-            hid[at] = hidden
+            hid[at] = (one * jax.nn.sigmoid(one) * three).astype(BF16)
+
+    def backward(layer, ex_dy, ex_gate, ex_du, ex_dgate):
+        @pl.loop(0, groups)
+        def _(group):
+            at = pl.ds(pl.multiple_of(group * rows, rows), rows)
             ex_gate.wait_recv(group)
             gate = rows_from_lanes(load_small(ex_gate.dst, group))
+            one, three = pre_act[at, 0:ffn], pre_act[at, ffn:2 * ffn]
+            sig = jax.nn.sigmoid(one)
             ex_dy.wait_recv(group)
             dyr = load_block(ex_dy.dst, group)
             proj = mm(dyr, w2[layer], NT)
-            gdy[at] = (gate * dyr.astype(F32)).astype(BF16)
             grad_h = gate * proj
             dact[at, 0:ffn] = (grad_h * three * sig * (1.0 + one * (1.0 - sig))).astype(BF16)
-            dact[at, ffn:2 * ffn] = (grad_h * act).astype(BF16)
+            dact[at, ffn:2 * ffn] = (grad_h * (one * sig)).astype(BF16)
             store_block(ex_du.src, group, mm(dact[at], w13[layer], NT))
             ex_du.start(group)
+            gdy[at] = (gate * dyr.astype(F32)).astype(BF16)
             store_small(ex_dgate.src, group,
-                        lanes_from_rows(jnp.sum(proj * hidden.astype(F32), axis=1, keepdims=True)))
+                        lanes_from_rows(jnp.sum(proj * hid[at].astype(F32), axis=1, keepdims=True)))
             ex_dgate.start(group)
 
     def partner_copy(src, dst, index):
@@ -343,20 +350,23 @@
             store.start()
         return stores
 
+    def gate_group(ex, slot_ref, route_ref, out_ref, group):
+        ex.wait_recv(group)
+        column = rows_from_lanes(load_small(ex.dst, group))
+        spread = jnp.where(pick_matrix(slot_ref, group), column, 0.0)
+        high, mid, low = [mm(row_of_step(), part) for part in split3(spread)]
+        per_step = (high + mid) + low
+        owner = shift(iota((size, n_tok), 0) + group * size, False, me)
+        for j in range(top_k):
+            here = route_ref[j:j + 1, :] == owner
+            out_ref[j:j + 1, :] += jnp.sum(jnp.where(here, per_step, 0.0), axis=0, keepdims=True)
+
     def gate_grads(ex, slot_ref, route_ref, out_ref):
         out_ref[...] = jnp.zeros(out_ref.shape, F32)
 
         @pl.loop(0, groups)
         def _(group):
-            ex.wait_recv(group)
-            column = rows_from_lanes(load_small(ex.dst, group))
-            spread = jnp.where(pick_matrix(slot_ref, group), column, 0.0)
-            high, mid, low = [mm(row_of_step(), part) for part in split3(spread)]
-            per_step = (high + mid) + low
-            owner = shift(iota((size, n_tok), 0) + group * size, False, me)
-            for j in range(top_k):
-                here = route_ref[j:j + 1, :] == owner
-                out_ref[j:j + 1, :] += jnp.sum(jnp.where(here, per_step, 0.0), axis=0, keepdims=True)
+            gate_group(ex, slot_ref, route_ref, out_ref, group)
 
     with jax.named_scope('make_plan_a'):
         make_plan(route_a, gate_a, slot_a, gt_a)
@@ -388,7 +398,8 @@
         fill(ex_dyb, slot_b, dy_ref)
     ex_oa.wait_sends()
     with jax.named_scope('backward_l1'):
-        backward(1, ex_xb, ex_dyb, ex_gb, ex_dub, ex_dgb, False)
+        recompute(1, ex_xb, False)
+        backward(1, ex_dyb, ex_gb, ex_dub, ex_dgb)
     ex_xb.wait_sends()
     with jax.named_scope('fill_xa2'):
         fill(ex_xa2, slot_a, x_ref)
@@ -409,15 +420,15 @@
         gate_grads(ex_dgb, slot_b, route_b, dgb_ref)
     ex_ob.wait_sends()
     with jax.named_scope('backward_l0'):
-        backward(0, ex_xa2, ex_dya, ex_ga, ex_dua, ex_dga, True)
+        recompute(0, ex_xa2, True)
+        backward(0, ex_dya, ex_ga, ex_dua, ex_dga)
     with jax.named_scope('weight_grads_l0'):
         sends_a = weight_grads(0)
     with jax.named_scope('finish_grads_l0'):
         stores_a = finish_grads(0, sends_a, dw1_a, dw3_a, dw2_a)
     with jax.named_scope('add_back_dua'):
-        add_back(ex_dua, slot_a, dy_mid, gx_ref)
-    with jax.named_scope('gate_grads_dga'):
-        gate_grads(ex_dga, slot_a, route_a, dga_ref)
+        dga_ref[...] = jnp.zeros(dga_ref.shape, F32)
+        add_back(ex_dua, slot_a, dy_mid, gx_ref, lambda group: gate_group(ex_dga, slot_a, route_a, dga_ref, group))
     for ex in (ex_dub, ex_xa2, ex_dya, ex_dua, ex_gb, ex_ga, ex_dgb, ex_dga):
         ex.wait_sends()
     for store in stores_b + stores_a:
@@ -431,8 +442,8 @@
     for read in reads:
         read.start()
     for k in (8, 9):
-        top_k = results[k].shape[1]
-        results[k][...] = sources[k][...].T[:, :top_k]
+        top_k = results[k].shape[0]
+        results[k][...] = sources[k][0:top_k, :]
     for read, write in zip(reads, writes):
         read.wait()
         write.start()
@@ -468,6 +479,7 @@
             pltpu.VMEM((2, ffn, dim), BF16),
             pltpu.VMEM((groups * rows, dim), BF16),
             pltpu.VMEM((groups * rows, ffn), BF16),
+            pltpu.VMEM((groups * rows, 2 * ffn), F32),
             pltpu.VMEM((groups * rows, 2 * ffn), BF16),
             pltpu.VMEM((groups * rows, dim), BF16),
             pltpu.VMEM((2, dim, 2 * ffn), F32),
@@ -491,8 +503,8 @@
             name='moe_step',
         )(x_start, grad_out, route_a.T, route_b.T, gate_a.T, gate_b.T, w1_a, w3_a, w2_a, w1_b, w3_b, w2_b)
         shapes = [jax.ShapeDtypeStruct(o.shape, o.dtype) for o in out[:8]]
-        pair = jax.ShapeDtypeStruct((n_tok, top_k), F32)
-        return pl.pallas_call(
+        pair = jax.ShapeDtypeStruct((top_k, n_tok), F32)
+        out = pl.pallas_call(
             write_kernel,
             out_shape=tuple(shapes) + (pair, pair),
             in_specs=[any_space] * 8 + [vmem] * 2,
@@ -500,6 +512,7 @@
             scratch_shapes=[pltpu.VMEM(o.shape, o.dtype) for o in out[:8]] + [dma((2, 8))],
             name='write_out',
         )(*out)
+        return tuple(out[:8]) + (out[8].T, out[9].T)
 
     return jax.shard_map(local_step, mesh=mesh,
                          in_specs=(tok_spec,) * 6 + (weight_spec,) * 6,

time: 346 us -> 340 us (0.983)
  no operation moved by 1% of the time
where the time goes in v3:
time: 340 us
  Pallas kernels  339 us (100%)
    pallas_call x1, Pallas kernels, local_step(): pl.pallas_call(functools.partial(moe_kernel, cfg), out_shape=(tok, tok, u...  335 us

profile of v3, /device:TPU:2, one launch (start us, length us, event | category | flops | bytes accessed | tf_op | source)
XLA Modules:
  0.0 339.8 jit_solution(14195545386308163799)
XLA Ops:
  0.6 335.0 %moe_step.1 = (bf16[256,512]{1,0:T(8,128)(2,1)}, bf16[256,512]{1,0:T(8,128)(2,1)}, f32[1,256,384]{2,1,0:T(8,128)}, f32[1,256,384]{2,1,0:T(8,128)}, f32[1,192,512...) custom-call(bf16[256,512]{1,0:T(8,128)(2,1)} %refs_0_.1, ...), custom_call_target="tpu_custom_call" | custom-call | tf_op jit(solution)/shard_map/moe_step/pallas_call | solution.py:496
  335.6 4.0 %write_out.1 = (bf16[256,512]{1,0:T(8,128)(2,1)}, bf16[256,512]{1,0:T(8,128)(2,1)}, f32[1,256,384]{2,1,0:T(8,128)}, f32[1,256,384]{2,1,0:T(8,128)}, f32[1,192,51...) custom-call(bf16[256,512]{1,0:T(8,128)(2,1)} %get-tuple-element.30.r, ...), custom_call_target="tpu_custom_call" | custom-call | tf_op jit(solution)/shard_map/write_out/pallas_call | solution.py:507

commit v4 on v3

--- a/solution.py
+++ b/solution.py
@@ -98,7 +98,7 @@
      xf_ref, gx_ref, dw1_a, dw3_a, dw2_a, dw1_b, dw3_b, dw2_b, dga_ref, dgb_ref,
      sa, sb, sc, sd, tx, ty, tz, ra, rb, rdb, rda,
      ga_s, ga_t, gb_s, gb_t, da_s, da_t, db_s, db_t,
-     slot_a, slot_b, gt_a, gt_b, acc, x_mid, dy_mid, w13, w2, xc, hid, pre_act, dact, gdy, dw13, dw2, in13, in2,
+     slot_a, slot_b, gt_a, gt_b, pick_a, pick_b, acc, x_mid, dy_mid, w13, w2, xc, hid, pre_act, dact, gdy, dw13, dw2, in13, in2,
      send_sems, recv_sems, gsend_sems, grecv_sems, load_sems, dp_send, dp_recv, out_sems) = refs
 
     me = lax.axis_index('ep')
@@ -226,11 +226,17 @@
     def load_small(ref, group):
         return group_slice(ref, group).reshape(size, 128)
 
-    def fill(ex, slot_ref, source, send=True):
-        @pl.loop(0, groups)
-        def _(group):
-            picked = pick_matrix(slot_ref, group).astype(F32).astype(BF16)
-            store_block(ex.src, group, mm(picked, source[...]))
+    def make_picks(slot_ref, pick_ref):
+        @pl.loop(0, groups)
+        def _(group):
+            at = pl.ds(pl.multiple_of(group * rows, rows), rows)
+            pick_ref[at] = pick_matrix(slot_ref, group).astype(F32).astype(BF16)
+
+    def fill(ex, pick_ref, source, send=True):
+        @pl.loop(0, groups)
+        def _(group):
+            at = pl.ds(pl.multiple_of(group * rows, rows), rows)
+            store_block(ex.src, group, mm(pick_ref[at], source[...]))
             if send:
                 ex.start(group)
 
@@ -370,8 +376,9 @@
 
     with jax.named_scope('make_plan_a'):
         make_plan(route_a, gate_a, slot_a, gt_a)
+        make_picks(slot_a, pick_a)
     with jax.named_scope('fill_xa'):
-        fill(ex_xa, slot_a, x_ref, send=False)
+        fill(ex_xa, pick_a, x_ref, send=False)
     with jax.named_scope('entry'):
         pl.semaphore_wait(barrier, n_exp)
 
@@ -381,6 +388,7 @@
 
     with jax.named_scope('make_plan_b'):
         make_plan(route_b, gate_b, slot_b, gt_b)
+        make_picks(slot_b, pick_b)
     for load in loads:
         load.wait()
     with jax.named_scope('forward_l0'):
@@ -388,21 +396,21 @@
     with jax.named_scope('mix_back_oa'):
         mix_back(ex_oa, slot_a, gt_a, x_ref, x_mid)
     with jax.named_scope('fill_xb'):
-        fill(ex_xb, slot_b, x_mid)
+        fill(ex_xb, pick_b, x_mid)
     with jax.named_scope('forward_l1'):
         forward(1, ex_xb, ex_ob)
     ex_xa.wait_sends()
     with jax.named_scope('fill_gates_gb'):
         fill_gates(ex_gb, slot_b, gt_b)
     with jax.named_scope('fill_dyb'):
-        fill(ex_dyb, slot_b, dy_ref)
+        fill(ex_dyb, pick_b, dy_ref)
     ex_oa.wait_sends()
     with jax.named_scope('backward_l1'):
         recompute(1, ex_xb, False)
         backward(1, ex_dyb, ex_gb, ex_dub, ex_dgb)
     ex_xb.wait_sends()
     with jax.named_scope('fill_xa2'):
-        fill(ex_xa2, slot_a, x_ref)
+        fill(ex_xa2, pick_a, x_ref)
     with jax.named_scope('fill_gates_ga'):
         fill_gates(ex_ga, slot_a, gt_a)
     with jax.named_scope('weight_grads_l1'):
@@ -411,7 +419,7 @@
     with jax.named_scope('add_back_dub'):
         add_back(ex_dub, slot_b, dy_ref, dy_mid)
     with jax.named_scope('fill_dya'):
-        fill(ex_dya, slot_a, dy_mid)
+        fill(ex_dya, pick_a, dy_mid)
     with jax.named_scope('mix_back_ob'):
         mix_back(ex_ob, slot_b, gt_b, x_mid, xf_ref)
     with jax.named_scope('finish_grads_l1'):
@@ -471,7 +479,7 @@
         block = [pltpu.VMEM((n_ep, 4 * MAIN + 16, 128), BF16)]
         lane = pltpu.VMEM((n_ep, 1, 128), F32)
         dma = pltpu.SemaphoreType.DMA
-        scratch = block * 11 + [lane] * 8 + [pltpu.VMEM((n_ep, n_tok), F32)] * 4 + [
+        scratch = block * 11 + [lane] * 8 + [pltpu.VMEM((n_ep, n_tok), F32)] * 4 + [pltpu.VMEM((groups * rows, n_tok), BF16)] * 2 + [
             pltpu.VMEM((n_tok, dim), F32),
             pltpu.VMEM((n_tok, dim), BF16),
             pltpu.VMEM((n_tok, dim), BF16),

time: 340 us -> 335 us (0.985); the launches traced: 340 us -> 331 us
  Pallas kernels: 339 us -> 330 us
    pallas_call x1, Pallas kernels: 335 us -> 326 us  [local_step(): pl.pallas_call(functools.partial(moe_kernel, cfg), out_shape=(tok, tok, u...]
where the time goes in v4:
time: 335 us; the launch traced here: 331 us
  Pallas kernels  330 us (99%)
    pallas_call x1, Pallas kernels, local_step(): pl.pallas_call(functools.partial(moe_kernel, cfg), out_shape=(tok, tok, u...  326 us

profile of v4, /device:TPU:2, one launch (start us, length us, event | category | flops | bytes accessed | tf_op | source)
XLA Modules:
  0.0 330.7 jit_solution(2075220212971403331)
XLA Ops:
  0.6 325.9 %moe_step.1 = (bf16[256,512]{1,0:T(8,128)(2,1)}, bf16[256,512]{1,0:T(8,128)(2,1)}, f32[1,256,384]{2,1,0:T(8,128)}, f32[1,256,384]{2,1,0:T(8,128)}, f32[1,192,512...) custom-call(bf16[256,512]{1,0:T(8,128)(2,1)} %refs_0_.1, ...), custom_call_target="tpu_custom_call" | custom-call | tf_op jit(solution)/shard_map/moe_step/pallas_call | solution.py:504
  326.5 4.0 %write_out.1 = (bf16[256,512]{1,0:T(8,128)(2,1)}, bf16[256,512]{1,0:T(8,128)(2,1)}, f32[1,256,384]{2,1,0:T(8,128)}, f32[1,256,384]{2,1,0:T(8,128)}, f32[1,192,51...) custom-call(bf16[256,512]{1,0:T(8,128)(2,1)} %get-tuple-element.30.r, ...), custom_call_target="tpu_custom_call" | custom-call | tf_op jit(solution)/shard_map/write_out/pallas_call | solution.py:515
